TPU v7x, 256 devices: a whole 4x4x8 slice. The times are simulated.
256 devices in a mesh: sample: 16 (over y, x), sy: 4 (over z_lo, core), sz: 4 (over z_hi).
Axes of the slice: x: 4, y: 4, z: 8 (z_hi: 4, z_lo: 2; z = z_hi * 2 + z_lo), core: 2. Of those that a mesh axis runs over, the one named last changes fastest.
Arguments:
- volume: bfloat16 [16, 32, 16, 32, 128], P('sample', None, 'sz', 'sy'), may hold values from -22.5 to 22.5
- amax_history: float32 [4, 16], replicated, may hold values from 0.48 to 2.5
- conv_first: bfloat16 [27, 32, 32], replicated, may hold values from -0.21875 to 0.21875
- conv_second: bfloat16 [27, 32, 32], replicated, may hold values from -0.21875 to 0.21875
- conv_third: bfloat16 [27, 64, 32], P(None, 'sy'), may hold values from -0.21875 to 0.21875
- conv_fourth: bfloat16 [27, 64, 64], P(None, 'sy'), may hold values from -0.15625 to 0.15625
- gain_fine: float32 [2, 32], replicated, may hold values from 0.5 to 1.5
- shift_fine: float32 [2, 32], replicated, may hold values from -0.5 to 0.5
- gain_coarse: float32 [2, 64], P(None, 'sy'), may hold values from 0.5 to 1.5
- shift_coarse: float32 [2, 64], P(None, 'sy'), may hold values from -0.5 to 0.5
Outputs:
- skip_features: bfloat16 [16, 32, 16, 32, 128], P('sample', None, 'sz', 'sy')
- coarse_features: bfloat16 [16, 64, 8, 1024], P('sample', 'sy', 'sz')
- amax_now: float32 [4], replicated
All inputs are finite; a program needn't handle non-finite values.
Results may differ from a plain program's by a relative error of at most 0.012.
Values may be sent and summed in bfloat16 or wider, within the bound.
A program may use at most 128 MiB of HBM per device.

v0:
```python
import jax
import jax.numpy as jnp
from jax import lax
from jax.sharding import Mesh
from jax.sharding import PartitionSpec as P

SY_SZ = ("sy_0", "sy_1", "sz")
SY = ("sy_0", "sy_1")
SAMPLE_SY_SZ = ("sample_0", "sample_1", "sy_0", "sy_1", "sz")
SAMPLE = ("sample_0", "sample_1")


norm_eps = 1e-05
leak_slope = 0.01


def padded_2(cells, sides, width):
    for axis, dim in sides:
        count = lax.axis_size(axis)
        ends = count - 1
        head = lax.slice_in_dim(cells, 0, width, axis=dim)
        tail = lax.slice_in_dim(cells, cells.shape[dim] - width, cells.shape[dim], axis=dim)
        cells = jnp.concatenate(
            [
                lax.ppermute(tail, axis, [(i, (i + 1) % count) for i in range(ends)]),
                cells,
                lax.ppermute(head, axis, [((i + 1) % count, i) for i in range(ends)]),
            ],
            axis=dim,
        )
    return cells


def copy_for_each(x, axis):
    copies = jnp.broadcast_to(x, (lax.axis_size(axis), *x.shape))
    return lax.all_to_all(copies, axis, split_axis=0, concat_axis=0, tiled=True)


def over_copies(x, axis):
    everything = copy_for_each(x, axis)
    return jnp.sum(everything, axis=0)


def packed_total(arrays, axis):
    flat, at, done = (jnp.concatenate([a.reshape(-1) for a in arrays]), 0, [])
    subtotal = over_copies(flat, axis)
    for a in arrays:
        done.append(subtotal[at : at + a.size].reshape(a.shape))
        at += a.size
    return tuple(done)


def one_axis_at_a_time(x, axes):
    for axis in axes:
        x = lax.pmax(x, axis)
    return x


def limited(values, bound):
    return jnp.clip(values.astype(jnp.float32), -bound, bound).astype(jnp.bfloat16)


def fine_faces(values):
    return padded_2(values, ((SY, 2), ("sz", 1)), 1)


def coarse_faces(values):
    return padded_2(values, (("sz", 1),), 1)


def fine_stats(values):
    flat_rows = values.reshape(values.shape[0], -1)
    return packed_total((jnp.sum(flat_rows, axis=1), jnp.sum(flat_rows * flat_rows, axis=1)), SY_SZ)


def coarse_stats(values):
    flat_rows = values.reshape(values.shape[0], -1)
    return packed_total((jnp.sum(flat_rows, axis=1), jnp.sum(flat_rows * flat_rows, axis=1)), "sz")


def apply_norm(values, moments, cell_count, gains, offset):
    chan_mean = moments[0] / cell_count
    spread = moments[1] / cell_count - chan_mean * chan_mean
    scaling = lax.rsqrt(spread + norm_eps) * gains
    shaped = (-1,) + (1,) * (values.ndim - 1)
    normed = (values - chan_mean.reshape(shaped)) * scaling.reshape(shaped) + offset.reshape(shaped)
    return jnp.where(normed >= 0, normed, leak_slope * normed).astype(jnp.bfloat16)


def level_one_conv(padded, weight):
    channels, depth_cells, height_cells, width_cells = padded.shape
    out_depth = depth_cells - 2
    out_height = height_cells - 2
    out_chan = weight.shape[1]
    widened = jnp.pad(padded, ((0, 0), (0, 0), (0, 0), (1, 1)))
    stacked = jnp.concatenate(
        [widened[:, :, :, x_tap : x_tap + width_cells] for x_tap in range(3)], axis=0
    )
    summed = jnp.zeros((out_chan, out_depth * out_height * width_cells), jnp.float32)
    for z_tap in range(3):
        for y_tap in range(3):
            first_tap = z_tap * 9 + y_tap * 3
            taps = weight[first_tap : first_tap + 3]
            matrix = jnp.transpose(taps, (1, 0, 2)).reshape(out_chan, 3 * channels)
            window = stacked[:, z_tap : z_tap + out_depth, y_tap : y_tap + out_height, :].reshape(
                3 * channels, -1
            )
            summed = summed + jnp.dot(matrix, window, preferred_element_type=jnp.float32)
    return summed.reshape(out_chan, out_depth, out_height, width_cells)


def level_two_conv(padded, weight, row_len):
    channels, depth_cells, flat_len = padded.shape
    out_depth = depth_cells - 2
    out_chan = weight.shape[1]
    column = lax.broadcasted_iota(jnp.int32, (1, 1, flat_len), 2) % row_len
    blank = jnp.zeros((), padded.dtype)
    sources = (
        jnp.where(column == row_len - 1, blank, padded),
        padded,
        jnp.where(column == 0, blank, padded),
    )
    wide_len = flat_len + 2 * row_len
    stacked = jnp.concatenate(
        [
            jnp.pad(sources[x_tap], ((0, 0), (0, 0), (row_len + 1, row_len + 1)))[
                :, :, x_tap : x_tap + wide_len
            ]
            for x_tap in range(3)
        ],
        axis=0,
    )
    summed = jnp.zeros((out_chan, out_depth * flat_len), jnp.float32)
    for z_tap in range(3):
        for y_tap in range(3):
            first_tap = z_tap * 9 + y_tap * 3
            taps = weight[first_tap : first_tap + 3]
            matrix = jnp.transpose(taps, (1, 0, 2)).reshape(out_chan, 3 * channels)
            window = stacked[
                :, z_tap : z_tap + out_depth, y_tap * row_len : y_tap * row_len + flat_len
            ].reshape(3 * channels, -1)
            summed = summed + jnp.dot(matrix, window, preferred_element_type=jnp.float32)
    return summed.reshape(out_chan, out_depth, flat_len)


def magnitude(values):
    return jnp.max(jnp.abs(values.astype(jnp.float32)))


def per_device(
    volume,
    amax_history,
    conv_first,
    conv_second,
    conv_third,
    conv_fourth,
    gain_fine,
    shift_fine,
    gain_coarse,
    shift_coarse,
):
    bounds = jnp.max(amax_history, axis=1)
    sample_count, channels, z_cells, y_cells, x_cells = volume.shape
    z_groups = lax.axis_size("sz")
    y_groups = lax.axis_size(SY)
    half_x = x_cells // 2
    half_z = z_cells // 2
    fine_cells = float(z_cells * z_groups * y_cells * y_groups * x_cells)
    coarse_cells = float(half_z * z_groups * (y_cells // 2) * y_groups * half_x)
    source = volume[0]
    layer_peaks = [magnitude(source)]
    first_in = limited(source, bounds[0])
    first_out = level_one_conv(fine_faces(first_in), conv_first)
    hidden = apply_norm(first_out, fine_stats(first_out), fine_cells, gain_fine[0], shift_fine[0])
    layer_peaks.append(magnitude(hidden))
    second_out = level_one_conv(fine_faces(limited(hidden, bounds[1])), conv_second)
    skip_out = apply_norm(
        second_out, fine_stats(second_out), fine_cells, gain_fine[1], shift_fine[1]
    )
    skip_list = [skip_out]
    blocks = skip_out.reshape(channels, half_z, 2, y_cells // 2, 2, half_x, 2)
    pooled = jnp.max(blocks, axis=(2, 4, 6))
    layer_peaks.append(magnitude(pooled))
    gathered = lax.all_gather(limited(pooled, bounds[2]), SY, axis=2, tiled=True)
    flat_in = gathered.reshape(channels, half_z, -1)
    third_out = level_two_conv(coarse_faces(flat_in), conv_third, half_x)
    coarse_hidden = apply_norm(
        third_out, coarse_stats(third_out), coarse_cells, gain_coarse[0], shift_coarse[0]
    )
    layer_peaks.append(magnitude(coarse_hidden))
    edged = coarse_faces(limited(coarse_hidden, bounds[3]))
    fourth_out = level_two_conv(lax.all_gather(edged, SY, axis=0, tiled=True), conv_fourth, half_x)
    coarse_list = [
        apply_norm(
            fourth_out, coarse_stats(fourth_out), coarse_cells, gain_coarse[1], shift_coarse[1]
        )
    ]
    peak_rows = [jnp.stack(layer_peaks)]
    peaks = jnp.max(jnp.stack(peak_rows), axis=0)
    peaks = one_axis_at_a_time(peaks, SAMPLE_SY_SZ)
    return (jnp.stack(skip_list), jnp.stack(coarse_list), peaks)


def solution(mesh):
    finer = Mesh(
        mesh.devices.reshape(4, 4, 2, 2, mesh.shape["sz"]),
        ("sample_0", "sample_1", "sy_0", "sy_1", "sz"),
    )
    return jax.shard_map(
        per_device,
        mesh=finer,
        in_specs=(
            P(SAMPLE, None, "sz", SY, None),
            P(),
            P(),
            P(),
            P(None, SY, None),
            P(None, SY, None),
            P(),
            P(),
            P(None, SY),
            P(None, SY),
        ),
        out_specs=(P(SAMPLE, None, "sz", SY, None), P(SAMPLE, SY, "sz", None), P()),
        check_vma=False,
    )
```

profile of v0, /device:TPU:1, one launch (start us, length us, event | category | flops | bytes accessed | tf_op | source)
XLA Modules:
  0.0 213.8 jit_solution(10618926767523013314)
XLA Ops:
  0.6 0.8 reduce_max.58
  1.4 0.7 fusion.85
  2.8 1.7 fusion.64
  4.5 4.9 %collective-permute-start = (bf16[32,4,1,128]{3,2,1,0:T(2,128)(2,1)S(1)}, bf16[32,4,1,128]{3,2,1,0:T(2,128)(2,1)S(1)}, u32[]{:S(2)}, u32[]{:S(2)}) collective-permute-start(bf16[32,4,1,128]{3,2,1,0:T(2,128)(2,1)S(1)} %get-tuple-element.53), channel_id=1, source_target_pairs={{0,4},{4,8},{8,12},{1,5},{5,9},{9,13},{2,6},{6,10},{10,14},{3,7},{... | collective-permute-start | bytes 98312 | tf_op jit(solution)/shard_map/ppermute | solution.py:25
  9.5 1.9 collective-permute-start.1
  11.4 0.9 slice_bitcast_fusion.36
  12.3 0.9 slice_bitcast_fusion.18
  13.2 0.9 slice_bitcast_fusion.9
  14.1 0.9 slice_bitcast_fusion.27
  15.2 4.9 %collective-permute-start.2 = (bf16[32,1,10,128]{3,2,1,0:T(8,128)(2,1)S(1)}, bf16[32,1,10,128]{3,2,1,0:T(8,128)(2,1)S(1)}, u32[]{:S(2)}, u32[]{:S(2)}) collective-permute-start(bf16[32,1,10,128]{3,2,1,0:T(8,128)(2,1)S(1)} %get-tuple-element.47), channel_id=1, source_target_pairs={{0,1},{1,2},{2,3},{4,5},{5,6},{6,7},{8,9},{9,10},{10,11},{12,13},{... | collective-permute-start | bytes 245768 | tf_op jit(solution)/shard_map/ppermute | solution.py:25
  20.1 1.3 collective-permute-start.3
  22.5 8.4 %collective-permute-done.3 = bf16[32,1,10,128]{3,2,1,0:T(8,128)(2,1)S(1)} collective-permute-done((bf16[32,1,10,128]{3,2,1,0:T(8,128)(2,1)S(1)}, bf16[32,1,10,128]{3,2,1,0:T(8,128)(2,1)S(1)}, u32[]{:S(2)}, u32[]{:S(2)}) %collective-permute-start.3) | collective-permute-done | bytes 81952 | tf_op jit(solution)/shard_map/ppermute | solution.py:27
  30.8 1.8 fusion.11
  33.0 1.2 pad_maximum_fusion
  34.2 1.5 fusion.77
  39.1 0.5 fusion.61
  39.8 0.6 broadcast_in_dim.48
  40.4 6.1 %all-to-all-start = ((f32[16,1,64]{2,1,0:T(1,128)}), f32[16,1,64]{2,1,0:T(1,128)S(1)}, u32[]{:S(2)}, u32[]{:S(2)}) async-start(f32[16,1,64]{2,1,0:T(1,128)} %broadcast_in_dim.48), calls=%async_computation | async-start | bytes 16384 | tf_op jit(solution)/shard_map/all_to_all | solution.py:36
  47.4 6.2 %all-to-all-done = f32[16,1,64]{2,1,0:T(1,128)S(1)} async-done(((f32[16,1,64]{2,1,0:T(1,128)}), f32[16,1,64]{2,1,0:T(1,128)S(1)}, u32[]{:S(2)}, u32[]{:S(2)}) %all-to-all-start) | async-done | bytes 4128 | tf_op jit(solution)/shard_map/all_to_all | solution.py:36
  53.6 0.9 minimum_convert_fusion
  54.6 2.8 %collective-permute-start.4 = (bf16[32,4,1,128]{3,2,1,0:T(2,128)(2,1)S(1)}, bf16[32,4,1,128]{3,2,1,0:T(2,128)(2,1)S(1)}, u32[]{:S(2)}, u32[]{:S(2)}) collective-permute-start(bf16[32,4,1,128]{3,2,1,0:T(2,128)(2,1)S(1)} %get-tuple-element.51), channel_id=1, source_target_pairs={{0,4},{4,8},{8,12},{1,5},{5,9},{9,13},{2,6},{6,10},{10,14},{3,7},{... | collective-permute-start | bytes 98312 | tf_op jit(solution)/shard_map/ppermute | solution.py:25
  57.4 1.9 collective-permute-start.5
  59.3 0.7 fusion.57
  61.0 2.0 collective-permute-done.5
  63.1 2.2 %collective-permute-start.6 = (bf16[32,1,10,128]{3,2,1,0:T(8,128)(2,1)S(1)}, bf16[32,1,10,128]{3,2,1,0:T(8,128)(2,1)S(1)}, u32[]{:S(2)}, u32[]{:S(2)}) collective-permute-start(bf16[32,1,10,128]{3,2,1,0:T(8,128)(2,1)S(1)} %get-tuple-element.45), channel_id=1, source_target_pairs={{0,1},{1,2},{2,3},{4,5},{5,6},{6,7},{8,9},{9,10},{10,11},{12,13},{... | collective-permute-start | bytes 245768 | tf_op jit(solution)/shard_map/ppermute | solution.py:25
  65.4 1.5 collective-permute-start.7
  67.3 6.3 %collective-permute-done.7 = bf16[32,1,10,128]{3,2,1,0:T(8,128)(2,1)S(1)} collective-permute-done((bf16[32,1,10,128]{3,2,1,0:T(8,128)(2,1)S(1)}, bf16[32,1,10,128]{3,2,1,0:T(8,128)(2,1)S(1)}, u32[]{:S(2)}, u32[]{:S(2)}) %collective-permute-start.7) | collective-permute-done | bytes 81952 | tf_op jit(solution)/shard_map/ppermute | solution.py:27
  73.6 1.8 select_maximum_fusion
  75.8 1.2 pad_maximum_fusion.1
  77.0 1.5 fusion.76
  81.8 0.5 multiply_reduce_fusion
  82.6 0.6 broadcast_in_dim.49
  83.2 5.1 %all-to-all-start.1 = ((f32[16,1,64]{2,1,0:T(1,128)}), f32[16,1,64]{2,1,0:T(1,128)S(1)}, u32[]{:S(2)}, u32[]{:S(2)}) async-start(f32[16,1,64]{2,1,0:T(1,128)} %broadcast_in_dim.49), calls=%async_computation.1 | async-start | bytes 16384 | tf_op jit(solution)/shard_map/all_to_all | solution.py:36
  91.2 0.6 copy.295
  91.8 3.4 %all-to-all-done.1 = f32[16,1,64]{2,1,0:T(1,128)S(1)} async-done(((f32[16,1,64]{2,1,0:T(1,128)}), f32[16,1,64]{2,1,0:T(1,128)S(1)}, u32[]{:S(2)}, u32[]{:S(2)}) %all-to-all-start.1) | async-done | bytes 4128 | tf_op jit(solution)/shard_map/all_to_all | solution.py:36
  95.4 2.9 %fusion.16 = bf16[32,2,4,64]{0,3,2,1:T(8,128)(2,1)S(1)} fusion(f32[32]{0:T(128)S(1)} %get-tuple-element.97, f32[32]{0:T(128)S(1)} %get-tuple-element.108, f32[32,2,2,4,2,64,2]{0,6,5,4,3,2,1:T(2,128)S(1)} %bitcast.326, f32[32]{0:T(128)S(1)} %get-tuple-element.107), kind=kLoop, calls=%fused_computation.59 | loop fusion | flops 1032192 | bytes 557440 | tf_op jit(solution)/shard_map/reduce_max | solution.py:182
  98.4 0.7 fusion.66
  99.1 6.3 %all_gather.6 = bf16[32,2,16,64]{3,0,1,2:T(8,128)(2,1)S(1)} all-gather(bf16[32,2,4,64]{3,0,1,2:T(8,128)(2,1)S(1)} %copy.297), channel_id=1, replica_groups=mesh['sample_0'=4,'sample_1'=4,'sy_0'=2,'sy_1'=2,'sz'=4] {'sy_0','sy_1'}, dimensions={2}, use_global_device_ids=true | all-gather | bytes 163840 | tf_op jit(solution)/shard_map/all_gather | solution.py:184
  105.8 2.2 %collective-permute-start.8 = (bf16[32,1,1024]{2,0,1:T(8,128)(2,1)S(1)}, bf16[32,1,1024]{2,0,1:T(8,128)(2,1)S(1)}, u32[]{:S(2)}, u32[]{:S(2)}) collective-permute-start(bf16[32,1,1024]{2,0,1:T(8,128)(2,1)S(1)} %get-tuple-element.74), channel_id=1, source_target_pairs={{0,1},{1,2},{2,3},{4,5},{5,6},{6,7},{8,9},{9,10},{10,11},{12,13},{... | collective-permute-start | bytes 196616 | tf_op jit(solution)/shard_map/ppermute | solution.py:25
  108.0 0.8 abs_reduce_fusion
  108.8 1.3 collective-permute-start.9
  110.1 6.8 %collective-permute-done.9 = bf16[32,1,1024]{2,0,1:T(8,128)(2,1)S(1)} collective-permute-done((bf16[32,1,1024]{2,0,1:T(8,128)(2,1)S(1)}, bf16[32,1,1024]{2,0,1:T(8,128)(2,1)S(1)}, u32[]{:S(2)}, u32[]{:S(2)}) %collective-permute-start.9) | collective-permute-done | bytes 65568 | tf_op jit(solution)/shard_map/ppermute | solution.py:27
  117.4 0.6 slice_bitcast_fusion
  120.3 0.6 broadcast_in_dim.55
  120.9 4.0 %all-to-all-start.2 = ((f32[4,1,32]{2,1,0:T(1,128)}), f32[4,1,32]{2,1,0:T(1,128)S(1)}, u32[]{:S(2)}, u32[]{:S(2)}) async-start(f32[4,1,32]{2,1,0:T(1,128)} %broadcast_in_dim.55), calls=%async_computation.2 | async-start | bytes 4096 | tf_op jit(solution)/shard_map/all_to_all | solution.py:36
  124.9 0.7 fusion.67
  125.7 5.6 %all-to-all-done.2 = f32[4,1,32]{2,1,0:T(1,128)S(1)} async-done(((f32[4,1,32]{2,1,0:T(1,128)}), f32[4,1,32]{2,1,0:T(1,128)S(1)}, u32[]{:S(2)}, u32[]{:S(2)}) %all-to-all-start.2) | async-done | bytes 544 | tf_op jit(solution)/shard_map/all_to_all | solution.py:36
  131.5 0.7 abs_reduce_fusion.1
  132.2 0.9 minimum_convert_fusion.1
  133.2 2.2 %collective-permute-start.10 = (bf16[16,1,1024]{2,1,0:T(2,128)(2,1)S(1)}, bf16[16,1,1024]{2,1,0:T(2,128)(2,1)S(1)}, u32[]{:S(2)}, u32[]{:S(2)}) collective-permute-start(bf16[16,1,1024]{2,1,0:T(2,128)(2,1)S(1)} %get-tuple-element.93), channel_id=1, source_target_pairs={{0,1},{1,2},{2,3},{4,5},{5,6},{6,7},{8,9},{9,10},{10,11},{12,13},{... | collective-permute-start | bytes 98312 | tf_op jit(solution)/shard_map/ppermute | solution.py:25
  135.4 1.3 collective-permute-start.11
  136.7 2.6 %pad_maximum_fusion.15 = f32[4]{0:T(128)S(1)} fusion(f32[1]{0:T(128)} %bitcast.61, f32[1]{0:T(128)} %bitcast.60, f32[1]{0:T(128)} %bitcast.59, f32[1]{0:T(128)} %bitcast.58), kind=kLoop, calls=%fused_computation.207 | loop fusion | flops 12 | bytes 32 | tf_op jit(solution)/shard_map/stack | solution.py:198
  139.4 8.7 %pmax.35 = f32[4]{0:T(128)S(1)} all-reduce(f32[4]{0:T(128)S(1)} %pad_maximum_fusion.15), channel_id=1, replica_groups=mesh['sample_0'=4,'sample_1'=4,'sy_0'=2,'sy_1'=2,'sz'=4] {'sample_0'}, use_global_device_ids=true, to_apply=%region_18.19 | all-reduce | flops 4 | bytes 32 | tf_op jit(solution)/shard_map/pmax | solution.py:55
  148.1 8.5 %pmax.36 = f32[4]{0:T(128)S(1)} all-reduce(f32[4]{0:T(128)S(1)} %pmax.35), channel_id=1, replica_groups=mesh['sample_0'=4,'sample_1'=4,'sy_0'=2,'sy_1'=2,'sz'=4] {'sample_1'}, use_global_device_ids=true, to_apply=%region_19.20 | all-reduce | flops 4 | bytes 32 | tf_op jit(solution)/shard_map/pmax | solution.py:55
  156.7 3.8 %pmax.37 = f32[4]{0:T(128)S(1)} all-reduce(f32[4]{0:T(128)S(1)} %pmax.36), channel_id=1, replica_groups=mesh['sample_0'=4,'sample_1'=4,'sy_0'=2,'sy_1'=2,'sz'=4] {'sy_0'}, use_global_device_ids=true, to_apply=%region_20.21 | all-reduce | flops 4 | bytes 32 | tf_op jit(solution)/shard_map/pmax | solution.py:55
  160.5 9.6 %pmax.38 = f32[4]{0:T(128)S(1)} all-reduce(f32[4]{0:T(128)S(1)} %pmax.37), channel_id=1, replica_groups=mesh['sample_0'=4,'sample_1'=4,'sy_0'=2,'sy_1'=2,'sz'=4] {'sy_1'}, use_global_device_ids=true, to_apply=%region_21.22 | all-reduce | flops 4 | bytes 32 | tf_op jit(solution)/shard_map/pmax | solution.py:55
  170.4 7.3 %all_gather.7 = bf16[64,4,1024]{2,1,0:T(4,128)(2,1)S(1)} all-gather(bf16[16,4,1024]{2,1,0:T(4,128)(2,1)S(1)} %pad_maximum_fusion.10), channel_id=1, replica_groups=mesh['sample_0'=4,'sample_1'=4,'sy_0'=2,'sy_1'=2,'sz'=4] {'sy_0','sy_1'}, dimensions={0}, use_global_device_ids=true | all-gather | bytes 655360 | tf_op jit(solution)/shard_map/all_gather | solution.py:192
  179.4 3.0 %pad_maximum_fusion.2 = bf16[192,4,1152]{2,1,0:T(4,128)(2,1)S(1)} fusion(bf16[64,4,1152]{2,1,0:T(4,128)(2,1)S(1)} %pad_slice_fusion, bf16[64,4,1152]{2,1,0:T(4,128)(2,1)S(1)} %pad_slice_fusion.1, bf16[64,4,1152]{2,1,0:T(4,128)(2,1)S(1)} %pad_slice_fusion.2), kind=kLoop, calls=%fused_computation.39 | loop fusion | flops 1769472 | bytes 3538944 | tf_op jit(solution)/shard_map/concatenate | solution.py:124
  182.4 8.0 %fusion.78 = (bf16[192,2,1024]{2,1,0:T(2,128)(2,1)S(1)}, bf16[192,2,1024]{2,1,0:T(2,128)(2,1)S(1)}, bf16[192,2,1024]{2,1,0:T(2,128)(2,1)S(1)}, bf16[192,2,1024]{...) fusion(bf16[192,4,1152]{2,1,0:T(4,128)(2,1)S(1)} %pad_maximum_f, ...), kind=kLoop, calls=%fused_computation.222 | loop fusion | bytes 14155776 | tf_op jit(solution)/shard_map/slice | solution.py:139
  194.6 0.6 broadcast_in_dim.57
  195.1 5.7 %all-to-all-start.3 = ((f32[4,1,32]{2,1,0:T(1,128)}), f32[4,1,32]{2,1,0:T(1,128)S(1)}, u32[]{:S(2)}, u32[]{:S(2)}) async-start(f32[4,1,32]{2,1,0:T(1,128)} %broadcast_in_dim.57), calls=%async_computation.3 | async-start | bytes 4096 | tf_op jit(solution)/shard_map/all_to_all | solution.py:36
  200.9 0.9 fusion.59
  201.8 10.9 %pmax.39 = f32[4]{0:T(128)} all-reduce(f32[4]{0:T(128)S(1)} %pmax.38), channel_id=1, replica_groups=mesh['sample_0'=4,'sample_1'=4,'sy_0'=2,'sy_1'=2,'sz'=4] {'sz'}, use_global_device_ids=true, to_apply=%region_22.23 | all-reduce | flops 4 | bytes 32 | tf_op jit(solution)/shard_map/pmax | solution.py:55
  212.9 0.9 fusion.70
  (191 shorter events, 22.6 us)
Async XLA Ops:
  0.6 20.8 %copy-start.3 = (f32[2,32]{1,0:T(2,128)S(1)}, f32[2,32]{1,0:T(2,128)}, u32[]{:S(2)}) copy-start(f32[2,32]{1,0:T(2,128)} %param.17) | copy-start | bytes 772
  4.5 10.4 %collective-permute-start = (bf16[32,4,1,128]{3,2,1,0:T(2,128)(2,1)S(1)}, bf16[32,4,1,128]{3,2,1,0:T(2,128)(2,1)S(1)}, u32[]{:S(2)}, u32[]{:S(2)}) collective-permute-start(bf16[32,4,1,128]{3,2,1,0:T(2,128)(2,1)S(1)} %get-tuple-element.53), channel_id=1, source_target_pairs={{0,4},{4,8},{8,12},{1,5},{5,9},{9,13},{2,6},{6,10},{10,14},{3,7},{... | collective-permute-start | bytes 98312 | tf_op jit(solution)/shard_map/ppermute | solution.py:25
  9.5 5.6 %collective-permute-start.1 = (bf16[32,4,1,128]{3,2,1,0:T(2,128)(2,1)S(1)}, bf16[32,4,1,128]{3,2,1,0:T(2,128)(2,1)S(1)}, u32[]{:S(2)}, u32[]{:S(2)}) collective-permute-start(bf16[32,4,1,128]{3,2,1,0:T(2,128)(2,1)S(1)} %get-tuple-element.54), channel_id=1, source_target_pairs={{4,0},{8,4},{12,8},{5,1},{9,5},{13,9},{6,2},{10,6},{14,10},{7,3},{... | collective-permute-start | bytes 98312 | tf_op jit(solution)/shard_map/ppermute | solution.py:27
  15.2 7.2 %collective-permute-start.2 = (bf16[32,1,10,128]{3,2,1,0:T(8,128)(2,1)S(1)}, bf16[32,1,10,128]{3,2,1,0:T(8,128)(2,1)S(1)}, u32[]{:S(2)}, u32[]{:S(2)}) collective-permute-start(bf16[32,1,10,128]{3,2,1,0:T(8,128)(2,1)S(1)} %get-tuple-element.47), channel_id=1, source_target_pairs={{0,1},{1,2},{2,3},{4,5},{5,6},{6,7},{8,9},{9,10},{10,11},{12,13},{... | collective-permute-start | bytes 245768 | tf_op jit(solution)/shard_map/ppermute | solution.py:25
  20.1 10.7 %collective-permute-start.3 = (bf16[32,1,10,128]{3,2,1,0:T(8,128)(2,1)S(1)}, bf16[32,1,10,128]{3,2,1,0:T(8,128)(2,1)S(1)}, u32[]{:S(2)}, u32[]{:S(2)}) collective-permute-start(bf16[32,1,10,128]{3,2,1,0:T(8,128)(2,1)S(1)} %get-tuple-element.48), channel_id=1, source_target_pairs={{1,0},{2,1},{3,2},{5,4},{6,5},{7,6},{9,8},{10,9},{11,10},{13,12},{... | collective-permute-start | bytes 245768 | tf_op jit(solution)/shard_map/ppermute | solution.py:27
  38.6 7.9 %copy-start.4 = (f32[2,16]{1,0:T(2,128)S(1)}, f32[2,16]{1,0:T(2,128)}, u32[]{:S(2)}) copy-start(f32[2,16]{1,0:T(2,128)} %param.19) | copy-start | bytes 388
  38.6 14.9 %copy-start.1 = (f32[2,32]{1,0:T(2,128)S(1)}, f32[2,32]{1,0:T(2,128)}, u32[]{:S(2)}) copy-start(f32[2,32]{1,0:T(2,128)} %param.16) | copy-start | bytes 772
  39.1 20.3 %copy-start = (bf16[1,32,4,8,128]{4,3,2,1,0:T(8,128)(2,1)S(1)}, bf16[1,32,4,8,128]{4,3,2,1,0:T(8,128)(2,1)}, u32[]{:S(2)}) copy-start(bf16[1,32,4,8,128]{4,3,2,1,0:T(8,128)(2,1)} %param.10) | copy-start | bytes 786436
  40.4 13.1 %all-to-all-start = ((f32[16,1,64]{2,1,0:T(1,128)}), f32[16,1,64]{2,1,0:T(1,128)S(1)}, u32[]{:S(2)}, u32[]{:S(2)}) async-start(f32[16,1,64]{2,1,0:T(1,128)} %broadcast_in_dim.48), calls=%async_computation | async-start | bytes 16384 | tf_op jit(solution)/shard_map/all_to_all | solution.py:36
  54.6 6.4 %collective-permute-start.4 = (bf16[32,4,1,128]{3,2,1,0:T(2,128)(2,1)S(1)}, bf16[32,4,1,128]{3,2,1,0:T(2,128)(2,1)S(1)}, u32[]{:S(2)}, u32[]{:S(2)}) collective-permute-start(bf16[32,4,1,128]{3,2,1,0:T(2,128)(2,1)S(1)} %get-tuple-element.51), channel_id=1, source_target_pairs={{0,4},{4,8},{8,12},{1,5},{5,9},{9,13},{2,6},{6,10},{10,14},{3,7},{... | collective-permute-start | bytes 98312 | tf_op jit(solution)/shard_map/ppermute | solution.py:25
  57.4 5.6 %collective-permute-start.5 = (bf16[32,4,1,128]{3,2,1,0:T(2,128)(2,1)S(1)}, bf16[32,4,1,128]{3,2,1,0:T(2,128)(2,1)S(1)}, u32[]{:S(2)}, u32[]{:S(2)}) collective-permute-start(bf16[32,4,1,128]{3,2,1,0:T(2,128)(2,1)S(1)} %get-tuple-element.52), channel_id=1, source_target_pairs={{4,0},{8,4},{12,8},{5,1},{9,5},{13,9},{6,2},{10,6},{14,10},{7,3},{... | collective-permute-start | bytes 98312 | tf_op jit(solution)/shard_map/ppermute | solution.py:27
  63.1 4.2 %collective-permute-start.6 = (bf16[32,1,10,128]{3,2,1,0:T(8,128)(2,1)S(1)}, bf16[32,1,10,128]{3,2,1,0:T(8,128)(2,1)S(1)}, u32[]{:S(2)}, u32[]{:S(2)}) collective-permute-start(bf16[32,1,10,128]{3,2,1,0:T(8,128)(2,1)S(1)} %get-tuple-element.45), channel_id=1, source_target_pairs={{0,1},{1,2},{2,3},{4,5},{5,6},{6,7},{8,9},{9,10},{10,11},{12,13},{... | collective-permute-start | bytes 245768 | tf_op jit(solution)/shard_map/ppermute | solution.py:25
  65.4 8.2 %collective-permute-start.7 = (bf16[32,1,10,128]{3,2,1,0:T(8,128)(2,1)S(1)}, bf16[32,1,10,128]{3,2,1,0:T(8,128)(2,1)S(1)}, u32[]{:S(2)}, u32[]{:S(2)}) collective-permute-start(bf16[32,1,10,128]{3,2,1,0:T(8,128)(2,1)S(1)} %get-tuple-element.46), channel_id=1, source_target_pairs={{1,0},{2,1},{3,2},{5,4},{6,5},{7,6},{9,8},{10,9},{11,10},{13,12},{... | collective-permute-start | bytes 245768 | tf_op jit(solution)/shard_map/ppermute | solution.py:27
  83.2 12.1 %all-to-all-start.1 = ((f32[16,1,64]{2,1,0:T(1,128)}), f32[16,1,64]{2,1,0:T(1,128)S(1)}, u32[]{:S(2)}, u32[]{:S(2)}) async-start(f32[16,1,64]{2,1,0:T(1,128)} %broadcast_in_dim.49), calls=%async_computation.1 | async-start | bytes 16384 | tf_op jit(solution)/shard_map/all_to_all | solution.py:36
  105.8 4.3 %collective-permute-start.8 = (bf16[32,1,1024]{2,0,1:T(8,128)(2,1)S(1)}, bf16[32,1,1024]{2,0,1:T(8,128)(2,1)S(1)}, u32[]{:S(2)}, u32[]{:S(2)}) collective-permute-start(bf16[32,1,1024]{2,0,1:T(8,128)(2,1)S(1)} %get-tuple-element.74), channel_id=1, source_target_pairs={{0,1},{1,2},{2,3},{4,5},{5,6},{6,7},{8,9},{9,10},{10,11},{12,13},{... | collective-permute-start | bytes 196616 | tf_op jit(solution)/shard_map/ppermute | solution.py:25
  108.8 8.1 %collective-permute-start.9 = (bf16[32,1,1024]{2,0,1:T(8,128)(2,1)S(1)}, bf16[32,1,1024]{2,0,1:T(8,128)(2,1)S(1)}, u32[]{:S(2)}, u32[]{:S(2)}) collective-permute-start(bf16[32,1,1024]{2,0,1:T(8,128)(2,1)S(1)} %get-tuple-element.73), channel_id=1, source_target_pairs={{1,0},{2,1},{3,2},{5,4},{6,5},{7,6},{9,8},{10,9},{11,10},{13,12},{... | collective-permute-start | bytes 196616 | tf_op jit(solution)/shard_map/ppermute | solution.py:27
  118.9 12.5 %copy-start.2 = (f32[2,16]{1,0:T(2,128)S(1)}, f32[2,16]{1,0:T(2,128)}, u32[]{:S(2)}) copy-start(f32[2,16]{1,0:T(2,128)} %param.18) | copy-start | bytes 388
  120.9 10.5 %all-to-all-start.2 = ((f32[4,1,32]{2,1,0:T(1,128)}), f32[4,1,32]{2,1,0:T(1,128)S(1)}, u32[]{:S(2)}, u32[]{:S(2)}) async-start(f32[4,1,32]{2,1,0:T(1,128)} %broadcast_in_dim.55), calls=%async_computation.2 | async-start | bytes 4096 | tf_op jit(solution)/shard_map/all_to_all | solution.py:36
  133.2 36.9 %collective-permute-start.10 = (bf16[16,1,1024]{2,1,0:T(2,128)(2,1)S(1)}, bf16[16,1,1024]{2,1,0:T(2,128)(2,1)S(1)}, u32[]{:S(2)}, u32[]{:S(2)}) collective-permute-start(bf16[16,1,1024]{2,1,0:T(2,128)(2,1)S(1)} %get-tuple-element.93), channel_id=1, source_target_pairs={{0,1},{1,2},{2,3},{4,5},{5,6},{6,7},{8,9},{9,10},{10,11},{12,13},{... | collective-permute-start | bytes 98312 | tf_op jit(solution)/shard_map/ppermute | solution.py:25
  135.4 34.7 %collective-permute-start.11 = (bf16[16,1,1024]{2,1,0:T(2,128)(2,1)S(1)}, bf16[16,1,1024]{2,1,0:T(2,128)(2,1)S(1)}, u32[]{:S(2)}, u32[]{:S(2)}) collective-permute-start(bf16[16,1,1024]{2,1,0:T(2,128)(2,1)S(1)} %get-tuple-element.94), channel_id=1, source_target_pairs={{1,0},{2,1},{3,2},{5,4},{6,5},{7,6},{9,8},{10,9},{11,10},{13,12},{... | collective-permute-start | bytes 98312 | tf_op jit(solution)/shard_map/ppermute | solution.py:27
  195.1 17.7 %all-to-all-start.3 = ((f32[4,1,32]{2,1,0:T(1,128)}), f32[4,1,32]{2,1,0:T(1,128)S(1)}, u32[]{:S(2)}, u32[]{:S(2)}) async-start(f32[4,1,32]{2,1,0:T(1,128)} %broadcast_in_dim.57), calls=%async_computation.3 | async-start | bytes 4096 | tf_op jit(solution)/shard_map/all_to_all | solution.py:36
where the time goes:
time: 215 us; the launch traced here: 214 us
  blocking collectives  55 us (26%)
  starting transfers between devices  49.4 us (23%)
  waiting for transfers between devices  39.2 us (18%)
  local copies, waits for them, and re-layouts  28.2 us (13%)
  other arithmetic  26.4 us (12%)
  matrix products  11.3 us (5%)
  between operations  4.17 us (2%)
    pmax x5, blocking collectives, one_axis_at_a_time(): x = lax.pmax(x, axis)  41.5 us
    ppermute x6, waiting for transfers between devices, padded_2(): lax.ppermute(head, axis, [((i + 1) % count, i) for i in range(ends)])  23.5 us
    all_to_all x4, starting transfers between devices, copy_for_each(): return lax.all_to_all(copies, axis, split_axis=0, concat_axis=0, tiled=True)  21 us
    ppermute x6, starting transfers between devices, padded_2(): lax.ppermute(tail, axis, [(i, (i + 1) % count) for i in range(ends)])  19.2 us
    all_to_all x4, waiting for transfers between devices, copy_for_each(): return lax.all_to_all(copies, axis, split_axis=0, concat_axis=0, tiled=True)  15.2 us
    ppermute x6, starting transfers between devices, padded_2(): lax.ppermute(head, axis, [((i + 1) % count, i) for i in range(ends)])  9.18 us
    slice x1, local copies, waits for them, and re-layouts, level_two_conv(): stacked[:, z_tap:z_tap + out_depth, y_tap * row_len:y_tap * row_len + fla...  8.01 us
    dot_general x18, matrix products, level_one_conv(): jnp.dot(matrix, window, preferred_element_type=jnp.float32)  7.55 us
  transfers between devices with their start and end apart: 16, of which 9 were waited for; matrix products, arithmetic and copies ran while one was open for 6% of the time, Pallas kernels for 0%

commit v1 on v0

v1 whole, which is shorter than its diff:
```python
import functools

import jax
import jax.numpy as jnp
from jax import lax
from jax.experimental import pallas as pl
from jax.experimental.pallas import tpu as pltpu
from jax.sharding import PartitionSpec as P

MESH = pl.DeviceIdType.MESH
F32 = jnp.float32
BF16 = jnp.bfloat16
EPS = 1e-05
SLOPE = 0.01
DIRS = ((-1, 0), (1, 0), (-1, -1), (-1, 1), (1, -1), (1, 1), (0, -1), (0, 1))


def body(
    ny, nz, gx, gy,
    vol, hist, w1, w2, w3, w4, gf, sf, gc, sc,
    skip, coarse, amax,
    vin, w1v, w2v, w3v, w4v, wf1, wf2, wg3, wg4,
    x1, r1, x2r, x2, r2, h3, p3, c3, h4, r4i, c4, a2a, a2s, gcol,
    st, am, outv, rows8,
    lsem, osem, hs, hr, ss, sr, ws, wr, gs, gr, bs, br, xs, xr,
):
    n = ny * nz
    sy = lax.axis_index("sy")
    sz = lax.axis_index("sz")
    smp = lax.axis_index("sample")
    me = sz * ny + sy
    mx_, my_ = lax.rem(smp, gx), lax.div(smp, gx)

    loads = [pltpu.make_async_copy(vol.at[:, z], vin.at[z], lsem.at[z]) for z in range(4)]
    for i, (s, d) in enumerate(((w1, w1v), (w2, w2v), (w3, w3v), (w4, w4v))):
        loads.append(pltpu.make_async_copy(s, d, lsem.at[4 + i]))
    for c in loads:
        c.start()

    def partner(d):
        p = lax.rem(me + d, n)
        return p, {"sy": lax.rem(p, ny), "sz": lax.div(p, ny)}

    order = sorted(range(1, n), key=lambda d: -min(d, n - d))
    barrier = pltpu.get_barrier_semaphore()
    for d in order:
        pl.semaphore_signal(barrier, inc=1, device_id=partner(d)[1], device_id_type=MESH)

    def xpeer(d):
        q = lax.rem(mx_ + d, gx)
        return q, {"sample": my_ * gx + q}

    def ypeer(d):
        q = lax.rem(my_ + d, gy)
        return q, {"sample": q * gx + mx_}

    for d in range(1, gx):
        pl.semaphore_signal(barrier, inc=1, device_id=xpeer(d)[1], device_id_type=MESH)
    for d in range(1, gy):
        pl.semaphore_signal(barrier, inc=1, device_id=ypeer(d)[1], device_id_type=MESH)

    def exists(dz, dy):
        cond = None
        for idx, cnt, d in ((sz, nz, dz), (sy, ny, dy)):
            if d == 0:
                continue
            c = (idx > 0) if d < 0 else (idx < cnt - 1)
            cond = c if cond is None else jnp.logical_and(cond, c)
        return cond

    lane = lax.broadcasted_iota(jnp.int32, (1, 128), 1)

    def bound_of(l):
        b = jnp.max(hist[l : l + 1, :], axis=1, keepdims=True)
        return b.astype(BF16).astype(F32)

    def src_z(dz, zl):
        return pl.ds(1, zl) if dz == 0 else (pl.ds(1, 1) if dz < 0 else pl.ds(zl, 1))

    def dst_z(dz, zl):
        return pl.ds(1, zl) if dz == 0 else (pl.ds(zl + 1, 1) if dz < 0 else pl.ds(0, 1))

    def halo(ph, buf, zl, yl, i):
        dz, dy = DIRS[i]
        return pltpu.make_async_remote_copy(
            src_ref=buf.at[src_z(dz, zl), src_z(dy, yl)],
            dst_ref=buf.at[dst_z(dz, zl), dst_z(dy, yl)],
            send_sem=hs.at[ph, i],
            recv_sem=hr.at[ph, i],
            device_id={"sy": sy + dy, "sz": sz + dz},
            device_id_type=MESH,
        )

    def halo_send(ph, buf, zl, yl, which):
        for i in which:
            @pl.when(exists(*DIRS[i]))
            def _():
                halo(ph, buf, zl, yl, i).start()

    def halo_wait(ph, buf, zl, yl, which):
        for i in which:
            @pl.when(exists(-DIRS[i][0], -DIRS[i][1]))
            def _():
                halo(ph, buf, zl, yl, i).wait_recv()

    def halo_done(ph, buf, zl, yl):
        for i in range(8):
            @pl.when(exists(*DIRS[i]))
            def _():
                halo(ph, buf, zl, yl, i).wait_send()

    def slots(d, length):
        return range(1, length + 1) if d == 0 else ((0,) if d > 0 else (length + 1,))

    def stat_copy(ph, d, src):
        p, dev = partner(d)
        return pltpu.make_async_remote_copy(
            src_ref=st.at[ph, me],
            dst_ref=st.at[ph, src],
            send_sem=ss.at[ph, d],
            recv_sem=sr.at[ph, src],
            device_id=dev,
            device_id_type=MESH,
        )

    def stat_send(ph, rows):
        st[ph, me] = rows
        for d in order:
            stat_copy(ph, d, me).start()

    def stat_wait(ph):
        for d in order:
            stat_copy(ph, d, partner(d)[0]).wait_recv()
        return st[ph]

    def to_rows(cols):
        return jnp.transpose(cols)

    def to_cols(row):
        return jnp.transpose(jnp.broadcast_to(row, (128, 128)))

    def affine(tot, totsq, cells, g, s):
        m = tot / cells
        var = totsq / cells - m * m
        a = lax.rsqrt(var + EPS) * g
        return a, m, s

    def act(v, aff):
        a, m, s = aff
        t = (v - m) * a + s
        return jnp.maximum(t, SLOPE * t)

    rows8[...] = jnp.zeros_like(rows8)
    rows8[0:2, 0:32] = gf[...]
    rows8[2:4, 0:32] = sf[...]
    rows8[4:6, 0:16] = gc[...]
    rows8[6:8, 0:16] = sc[...]
    gcols = jnp.transpose(rows8[...])

    def gain_col(j, count):
        return jnp.broadcast_to(gcols[0:count, j : j + 1], (count, 128))

    ri = lax.broadcasted_iota(jnp.int32, (256, 256), 0)
    ci = lax.broadcasted_iota(jnp.int32, (256, 256), 1)

    def onehot(cond):
        return jnp.where(cond, 1.0, 0.0).astype(BF16)

    into = onehot(jnp.logical_and((ri & 31) == (ci >> 3), (ri >> 5) == (ci & 7)))

    b0 = bound_of(0)
    for i in range(4):
        loads[i].wait()
    peak0 = jnp.zeros((256, 128), F32)
    for zp in range(2):
        parts = []
        for z in (2 * zp, 2 * zp + 1):
            v = vin[z].astype(F32).reshape(256, 128)
            peak0 = jnp.maximum(peak0, jnp.abs(v))
            parts.append(v.astype(BF16))
        moved = jnp.dot(into, jnp.concatenate(parts, axis=1), preferred_element_type=F32)
        moved = jnp.clip(moved, -b0, b0).astype(BF16)
        for k in range(2):
            for y in range(8):
                x1[1 + 2 * zp + k, 1 + y] = moved[32 * y : 32 * y + 32, 128 * k : 128 * k + 128]
    peak0 = jnp.max(jnp.max(peak0, axis=0, keepdims=True), axis=1, keepdims=True)

    pl.semaphore_wait(barrier, (n - 1) + (gx - 1) + (gy - 1))
    halo_send(0, x1, 4, 8, range(8))

    for i in range(4, 8):
        loads[i].wait()

    def lanes_of(w):
        return jnp.concatenate([w[k] for k in range(9)], axis=1)

    wf1[...] = lanes_of(w1v)
    wf2[...] = lanes_of(w2v)
    wg3[sy] = lanes_of(w3v)
    wg4[sy] = lanes_of(w4v)
    gcol[sy, 0] = gain_col(4, 16)
    gcol[sy, 1] = gain_col(6, 16)

    def zero_missing(buf, zl, yl):
        for i in range(8):
            dz, dy = DIRS[i]
            @pl.when(jnp.logical_not(exists(-dz, -dy)))
            def _():
                for z in slots(dz, zl):
                    for y in slots(dy, yl):
                        buf[z, y] = jnp.zeros(buf.shape[2:], buf.dtype)

    zero_missing(x1, 4, 8)

    first, last = lane == 0, lane == 127

    def combine(p0, p1, p2, lo, hi):
        left = jnp.where(lo, 0.0, pltpu.roll(p0, 1, 1))
        right = jnp.where(hi, 0.0, pltpu.roll(p2, 127, 1))
        return p1 + left + right

    def fine_conv(buf, w, z):
        strips = []
        for zt in range(3):
            blocks = [buf[z + zt, y] for y in range(10)]
            for yt in range(3):
                strips.append(jnp.concatenate(blocks[yt : yt + 8], axis=1))
        got = jnp.dot(w, jnp.concatenate(strips, axis=0), preferred_element_type=F32)
        outs = []
        for y in range(8):
            blk = got[:, 128 * y : 128 * y + 128]
            outs.append(combine(blk[0:32], blk[32:64], blk[64:96], first, last))
        return outs

    zero = jnp.zeros((32, 128), F32)

    def gather_stats(acc, blocks, extremes):
        s, q, hi, lo = acc
        for b in blocks:
            s = s + b
            q = q + b * b
            if extremes:
                hi = jnp.maximum(hi, b)
                lo = jnp.minimum(lo, b)
        return s, q, hi, lo

    def mixed_row(cols):
        t = to_rows(cols)
        total = jnp.sum(t, axis=0, keepdims=True)
        high = jnp.max(t, axis=0, keepdims=True)
        low = jnp.min(t, axis=0, keepdims=True)
        return jnp.where(lane < 64, total, jnp.where(lane < 96, high, low))

    def mixed_total(got):
        total = jnp.sum(got[:, 0:1, :], axis=0)
        high = jnp.max(got[:, 0:1, :], axis=0)
        low = jnp.min(got[:, 0:1, :], axis=0)
        return to_cols(jnp.where(lane < 64, total, jnp.where(lane < 96, high, low)))

    wa = wf1[...]
    acc = (zero, zero, jnp.full((32, 128), -jnp.inf, F32), jnp.full((32, 128), jnp.inf, F32))
    halo_wait(0, x1, 4, 8, (6, 7))
    for z in (1, 2):
        outs = fine_conv(x1, wa, z)
        acc = gather_stats(acc, outs, True)
        for y in range(8):
            r1[z, y] = outs[y]
        x2r[z + 1, 1] = outs[0].astype(BF16)
        x2r[z + 1, 8] = outs[7].astype(BF16)
    halo_wait(0, x1, 4, 8, range(6))
    for z in (0, 3):
        outs = fine_conv(x1, wa, z)
        acc = gather_stats(acc, outs, True)
        for y in range(8):
            r1[z, y] = outs[y]
            x2r[z + 1, y + 1] = outs[y].astype(BF16)
        halo_send(1, x2r, 4, 8, (0, 2, 3) if z == 0 else (1, 4, 5))
    halo_send(1, x2r, 4, 8, (6, 7))
    row = mixed_row(jnp.concatenate(acc, axis=0))
    stat_send(0, jnp.concatenate([row, jnp.broadcast_to(peak0, (1, 128))], axis=0))

    fine_cells = float(4 * nz * 8 * ny * 128)
    coarse_cells = fine_cells / 8

    def fine_affine(cols, j):
        return affine(cols[0:32], cols[32:64], fine_cells, gain_col(j, 32), gain_col(2 + j, 32))

    def peak_of(high, low, aff):
        v = jnp.maximum(jnp.abs(act(high, aff)), jnp.abs(act(low, aff))).astype(BF16).astype(F32)
        return jnp.max(jnp.max(v, axis=0, keepdims=True), axis=1, keepdims=True)

    got = stat_wait(0)
    peak0 = jnp.max(jnp.max(got[:, 1:2, :], axis=0), axis=1, keepdims=True)
    cols = mixed_total(got)
    aff = fine_affine(cols, 0)
    peak1 = peak_of(cols[64:96], cols[96:128], aff)
    b1 = bound_of(1)

    def settle(v, aff, b):
        return jnp.clip(act(v, aff), -b, b).astype(BF16)

    for z in range(4):
        for y in range(8):
            x2[z + 1, y + 1] = settle(r1[z, y], aff, b1)

    def settle_halo(ph, raw, buf, zl, yl, which, aff, b):
        for i in which:
            dz, dy = DIRS[i]
            there = exists(-dz, -dy)

            @pl.when(there)
            def _():
                halo(ph, raw, zl, yl, i).wait_recv()
                for z in slots(dz, zl):
                    for y in slots(dy, yl):
                        buf[z, y] = settle(raw[z, y].astype(F32), aff, b)

            @pl.when(jnp.logical_not(there))
            def _():
                for z in slots(dz, zl):
                    for y in slots(dy, yl):
                        buf[z, y] = jnp.zeros(buf.shape[2:], buf.dtype)

    wb = wf2[...]
    acc = (zero, zero, None, None)
    settle_halo(1, x2r, x2, 4, 8, (6, 7), aff, b1)
    for z in (1, 2):
        outs = fine_conv(x2, wb, z)
        acc = gather_stats(acc, outs, False)
        for y in range(8):
            r2[z, y] = outs[y]
    settle_halo(1, x2r, x2, 4, 8, range(6), aff, b1)

    def group(d, src, which):
        q = lax.rem(sy + d, ny)
        buf = (wg3, wg4, gcol)[which]
        return pltpu.make_async_remote_copy(
            src_ref=buf.at[sy], dst_ref=buf.at[src],
            send_sem=ws.at[which, d], recv_sem=wr.at[which, src],
            device_id={"sy": q}, device_id_type=MESH,
        )

    for which in range(3):
        for d in range(1, ny):
            group(d, sy, which).start()

    for z in (0, 3):
        outs = fine_conv(x2, wb, z)
        acc = gather_stats(acc, outs, False)
        for y in range(8):
            r2[z, y] = outs[y]

    s_r = lax.broadcasted_iota(jnp.int32, (256, 128), 0)
    s_c = lax.broadcasted_iota(jnp.int32, (256, 128), 1)
    pick = onehot(s_r == jnp.where(s_c < 64, 2 * s_c, 2 * s_c))
    highs, lows = [], []
    for zp in range(2):
        hrow, lrow = [], []
        for yp in range(4):
            m = jnp.maximum(
                jnp.maximum(r2[2 * zp, 2 * yp], r2[2 * zp, 2 * yp + 1]),
                jnp.maximum(r2[2 * zp + 1, 2 * yp], r2[2 * zp + 1, 2 * yp + 1]),
            )
            m = jnp.maximum(m, pltpu.roll(m, 127, 1))
            h = m.astype(BF16)
            hrow.append(h)
            lrow.append((m - h.astype(F32)).astype(BF16))
        highs.append(jnp.concatenate(hrow, axis=0))
        lows.append(jnp.concatenate(lrow, axis=0))
    pooled = jnp.dot(jnp.concatenate(highs, axis=1), pick, preferred_element_type=F32)
    pooled = pooled + jnp.dot(jnp.concatenate(lows, axis=1), pick, preferred_element_type=F32)
    hi = jnp.full((32, 128), -jnp.inf, F32)
    lo = jnp.full((32, 128), jnp.inf, F32)
    for yp in range(4):
        blk = pooled[32 * yp : 32 * yp + 32]
        p3[yp] = blk
        h3[1, yp + 1] = blk.astype(BF16)
        hi = jnp.maximum(hi, blk)
        lo = jnp.minimum(lo, blk)
    halo_send(2, h3, 1, 4, range(8))
    row = mixed_row(jnp.concatenate([acc[0], acc[1], hi, lo], axis=0))
    stat_send(1, jnp.concatenate([row, row], axis=0))

    got = stat_wait(1)
    cols = mixed_total(got)
    aff2 = fine_affine(cols, 1)
    peak2 = peak_of(cols[64:96], cols[96:128], aff2)
    b2 = bound_of(2)
    for yp in range(4):
        c3[1, yp + 1] = settle(p3[yp], aff2, b2)
    settle_halo(2, h3, c3, 1, 4, range(8), aff2, b2)

    lower = lane < 64
    cfirst, clast = (lane & 63) == 0, (lane & 63) == 63

    def coarse_conv(buf, w):
        strips = []
        mids = [buf[1, y] for y in range(6)]
        pairs = [[], mids, []]
        for y in range(6):
            own = mids[y].astype(F32)
            prev = buf[0, y].astype(F32)
            nxt = buf[2, y].astype(F32)
            pairs[0].append(pltpu.roll(jnp.where(lower, own, prev), 64, 1).astype(BF16))
            pairs[2].append(pltpu.roll(jnp.where(lower, nxt, own), 64, 1).astype(BF16))
        for zt in range(3):
            for yt in range(3):
                strips.append(jnp.concatenate(pairs[zt][yt : yt + 4], axis=1))
        got = jnp.dot(w, jnp.concatenate(strips, axis=0), preferred_element_type=F32)
        outs = []
        for y in range(4):
            blk = got[:, 128 * y : 128 * y + 128]
            parts = []
            for g in range(4):
                t = blk[48 * g : 48 * g + 48]
                parts.append(combine(t[0:16], t[16:32], t[32:48], cfirst, clast))
            outs.append(jnp.concatenate(parts, axis=0))
        return outs

    for d in range(1, ny):
        group(d, lax.rem(sy + d, ny), 0).wait_recv()
    outs = coarse_conv(c3, wg3[...].reshape(192, 288))
    zero64 = jnp.zeros((64, 128), F32)
    acc = (zero64, zero64, jnp.full((64, 128), -jnp.inf, F32), jnp.full((64, 128), jnp.inf, F32))
    acc = gather_stats(acc, outs, True)
    for y in range(4):
        h4[1, y + 1] = outs[y].astype(BF16)
        r4i[y] = outs[y]
    halo_send(3, h4, 1, 4, range(8))

    def double_rows(acc, extremes):
        t = to_rows(jnp.concatenate(acc[0:2], axis=0))
        r0 = jnp.sum(t, axis=0, keepdims=True)
        if not extremes:
            return jnp.concatenate([r0, r0], axis=0)
        t = to_rows(jnp.concatenate(acc[2:4], axis=0))
        high = jnp.max(t, axis=0, keepdims=True)
        low = jnp.min(t, axis=0, keepdims=True)
        return jnp.concatenate([r0, jnp.where(lower, high, low)], axis=0)

    stat_send(2, double_rows(acc, True))

    outof = onehot(jnp.logical_and((ci & 31) == (ri >> 3), (ci >> 5) == (ri & 7)))
    stores = []
    for zp in range(2):
        parts = []
        for z in (2 * zp, 2 * zp + 1):
            parts.append(jnp.concatenate([act(r2[z, y], aff2).astype(BF16) for y in range(8)], axis=0))
        moved = jnp.dot(outof, jnp.concatenate(parts, axis=1), preferred_element_type=F32)
        for k in range(2):
            z = 2 * zp + k
            outv[z] = moved[:, 128 * k : 128 * k + 128].reshape(32, 8, 128).astype(BF16)
            stores.append(pltpu.make_async_copy(outv.at[z], skip.at[:, z], osem.at[z]))
            stores[-1].start()

    for d in range(1, ny):
        group(d, lax.rem(sy + d, ny), 2).wait_recv()
    gall = gcol[...]
    got = stat_wait(2)
    cols = to_cols(jnp.sum(got[:, 0:1, :], axis=0))
    high = jnp.max(got[:, 1:2, :], axis=0)
    low = jnp.min(got[:, 1:2, :], axis=0)
    ext = to_cols(jnp.where(lower, high, low))
    aff3 = affine(cols[0:64], cols[64:128], coarse_cells, gall[:, 0].reshape(64, 128), gall[:, 1].reshape(64, 128))
    peak3 = peak_of(ext[0:64], ext[64:128], aff3)
    b3 = bound_of(3)

    peaks = jnp.where(lane == 0, peak0, jnp.where(lane == 1, peak1, jnp.where(lane == 2, peak2, peak3)))

    def cross(step, d, src):
        mine, peer = (mx_, xpeer) if step == 0 else (my_, ypeer)
        return pltpu.make_async_remote_copy(
            src_ref=am.at[step, mine], dst_ref=am.at[step, src],
            send_sem=xs.at[step, d], recv_sem=xr.at[step, src],
            device_id=peer(d)[1], device_id_type=MESH,
        )

    am[0, mx_] = peaks
    for d in range(1, gx):
        cross(0, d, mx_).start()

    for y in range(4):
        c4[1, y + 1] = settle(r4i[y], aff3, b3)
    settle_halo(3, h4, c4, 1, 4, range(8), aff3, b3)

    for d in range(1, ny):
        group(d, lax.rem(sy + d, ny), 1).wait_recv()
    outs = coarse_conv(c4, wg4[...].reshape(192, 576))
    acc = gather_stats((zero64, zero64, None, None), outs, False)
    for g in range(4):
        for y in range(4):
            a2s[g, y] = outs[y][16 * g : 16 * g + 16]

    def swap(d, src):
        q = lax.rem(sy + d, ny)
        return pltpu.make_async_remote_copy(
            src_ref=a2s.at[q], dst_ref=a2a.at[src],
            send_sem=bs.at[d], recv_sem=br.at[src],
            device_id={"sy": q}, device_id_type=MESH,
        )

    for d in range(1, ny):
        swap(d, sy).start()
    stat_send(3, double_rows(acc, False))
    a2a[sy] = a2s[sy]

    for d in range(1, gx):
        cross(0, d, xpeer(d)[0]).wait_recv()
    am[1, my_] = jnp.max(am[0, 0:gx], axis=0)
    for d in range(1, gy):
        cross(1, d, my_).start()

    for d in range(1, ny):
        swap(d, lax.rem(sy + d, ny)).wait_recv()
    got = stat_wait(3)
    rows8b = to_cols(jnp.sum(got[:, 0:1, :], axis=0))
    gs[...] = rows8b
    tot = gs[pl.ds(pl.multiple_of(sy * 16, 8), 16), :]
    totsq = gs[pl.ds(pl.multiple_of(64 + sy * 16, 8), 16), :]
    aff4 = affine(tot, totsq, coarse_cells, gain_col(5, 16), gain_col(7, 16))
    planes = [[], []]
    for g in range(4):
        for yp in range(2):
            u = act(a2a[g, 2 * yp], aff4)
            v = act(a2a[g, 2 * yp + 1], aff4)
            planes[0].append(jnp.where(lower, u, pltpu.roll(v, 64, 1)))
            planes[1].append(jnp.where(lower, pltpu.roll(u, 64, 1), v))
    for z in range(2):
        coarse[z] = jnp.concatenate(planes[z], axis=1).astype(BF16)

    for d in range(1, gy):
        cross(1, d, ypeer(d)[0]).wait_recv()
    amax[...] = jnp.max(am[1, 0:gy], axis=0)

    for c in stores:
        c.wait()
    halo_done(0, x1, 4, 8)
    halo_done(1, x2r, 4, 8)
    halo_done(2, h3, 1, 4)
    halo_done(3, h4, 1, 4)
    for ph in range(4):
        for d in order:
            stat_copy(ph, d, me).wait_send()
    for which in range(3):
        for d in range(1, ny):
            group(d, sy, which).wait_send()
    for d in range(1, ny):
        swap(d, sy).wait_send()
    for d in range(1, gx):
        cross(0, d, mx_).wait_send()
    for d in range(1, gy):
        cross(1, d, my_).wait_send()


def solution(mesh):
    ny, nz, ns = mesh.shape["sy"], mesh.shape["sz"], mesh.shape["sample"]
    gx = 4 if ns % 4 == 0 else ns
    gy = ns // gx
    n = ny * nz
    vmem = pl.BlockSpec(memory_space=pltpu.VMEM)
    hbm = pl.BlockSpec(memory_space=pl.ANY)

    def step(volume, hist, w1, w2, w3, w4, gf, sf, gc, sc):
        dma = pltpu.SemaphoreType.DMA
        skip, coarse, amax = pl.pallas_call(
            functools.partial(body_entry, ny, nz, gx, gy),
            out_shape=(
                jax.ShapeDtypeStruct((32, 4, 8, 128), BF16),
                jax.ShapeDtypeStruct((2, 16, 1024), BF16),
                jax.ShapeDtypeStruct((1, 128), F32),
            ),
            in_specs=[hbm, vmem, hbm, hbm, hbm, hbm, vmem, vmem, vmem, vmem],
            out_specs=(hbm, vmem, vmem),
            scratch_shapes=[
                pltpu.VMEM((4, 32, 8, 128), BF16),
                pltpu.VMEM((9, 96, 32), BF16),
                pltpu.VMEM((9, 96, 32), BF16),
                pltpu.VMEM((9, 48, 32), BF16),
                pltpu.VMEM((9, 48, 64), BF16),
                pltpu.VMEM((96, 288), BF16),
                pltpu.VMEM((96, 288), BF16),
                pltpu.VMEM((ny, 48, 288), BF16),
                pltpu.VMEM((ny, 48, 576), BF16),
                pltpu.VMEM((6, 10, 32, 128), BF16),
                pltpu.VMEM((4, 8, 32, 128), F32),
                pltpu.VMEM((6, 10, 32, 128), BF16),
                pltpu.VMEM((6, 10, 32, 128), BF16),
                pltpu.VMEM((4, 8, 32, 128), F32),
                pltpu.VMEM((3, 6, 32, 128), BF16),
                pltpu.VMEM((4, 32, 128), F32),
                pltpu.VMEM((3, 6, 32, 128), BF16),
                pltpu.VMEM((3, 6, 64, 128), BF16),
                pltpu.VMEM((4, 64, 128), F32),
                pltpu.VMEM((3, 6, 64, 128), BF16),
                pltpu.VMEM((ny, 4, 16, 128), F32),
                pltpu.VMEM((ny, 4, 16, 128), F32),
                pltpu.VMEM((ny, 2, 16, 128), F32),
                pltpu.VMEM((4, n, 2, 128), F32),
                pltpu.VMEM((2, 4, 1, 128), F32),
                pltpu.VMEM((4, 32, 8, 128), BF16),
                pltpu.VMEM((8, 128), F32),
                pltpu.VMEM((128, 128), F32),
                dma((8,)),
                dma((4,)),
                dma((4, 8)),
                dma((4, 8)),
                dma((4, n)),
                dma((4, n)),
                dma((3, ny)),
                dma((3, ny)),
                dma((ny,)),
                dma((ny,)),
                dma((2, 4)),
                dma((2, 4)),
            ],
            compiler_params=pltpu.CompilerParams(collective_id=0, has_side_effects=True),
            name="encoder",
        )(
            volume.reshape(32, 4, 8, 128), hist, w1.reshape(9, 96, 32), w2.reshape(9, 96, 32),
            w3.reshape(9, 48, 32), w4.reshape(9, 48, 64), gf, sf, gc, sc,
        )
        return (
            skip.reshape(1, 32, 4, 8, 128),
            jnp.transpose(coarse, (1, 0, 2)).reshape(1, 16, 2, 1024),
            amax[0, :4],
        )

    return jax.shard_map(
        step,
        mesh=mesh,
        in_specs=(
            P("sample", None, "sz", "sy", None), P(), P(), P(),
            P(None, "sy", None), P(None, "sy", None), P(), P(), P(None, "sy"), P(None, "sy"),
        ),
        out_specs=(P("sample", None, "sz", "sy", None), P("sample", "sy", "sz", None), P()),
        check_vma=False,
    )


def body_entry(ny, nz, gx, gy, *refs):
    (
        vol, hist, w1, w2, w3, w4, gf, sf, gc, sc, skip, coarse, amax,
        vin, w1v, w2v, w3v, w4v, wf1, wf2, wg3, wg4,
        x1, r1, x2r, x2, r2, h3, p3, c3, h4, r4i, c4, a2a, a2s, gcol,
        st, am, outv, rows8, tcols,
        lsem, osem, hs, hr, ss, sr, ws, wr, bs, br, xs, xr,
    ) = refs
    body(
        ny, nz, gx, gy,
        vol, hist, w1, w2, w3, w4, gf, sf, gc, sc, skip, coarse, amax,
        vin, w1v, w2v, w3v, w4v, wf1, wf2, wg3, wg4,
        x1, r1, x2r, x2, r2, h3, p3, c3, h4, r4i, c4, a2a, a2s, gcol,
        st, am, outv, rows8,
        lsem, osem, hs, hr, ss, sr, ws, wr, tcols, None, bs, br, xs, xr,
    )
```

time: 215 us -> 57.5 us (0.27)
  blocking collectives: 55 us -> 0 us
  Pallas kernels: 0 us -> 52.9 us
  starting transfers between devices: 49.4 us -> 0 us
  waiting for transfers between devices: 39.2 us -> 0 us
  other arithmetic: 26.4 us -> 0 us
  local copies, waits for them, and re-layouts: 28.2 us -> 3.72 us
  matrix products: 11.3 us -> 0 us
  between operations: 4.17 us -> 0.65 us
    pallas_call x0 -> x1, Pallas kernels: none -> 52.9 us  [step(): pl.pallas_call(functools.partial(body_entry, ny, nz, gx, gy), out_shape=(...]
    pmax x5 -> x0, blocking collectives: 41.5 us -> none  [one_axis_at_a_time(): x = lax.pmax(x, axis)]
    ppermute x12 -> x0, starting transfers between devices: 28.4 us -> none  [the longest x6 19.2 us: padded_2(): lax.ppermute(tail, axis, [(i, (i + 1) % count) for i in range(ends)])]
    ppermute x12 -> x0, waiting for transfers between devices: 24 us -> none  [the longest x6 23.5 us: padded_2(): lax.ppermute(head, axis, [((i + 1) % count, i) for i in range(ends)])]
    all_to_all x4 -> x0, starting transfers between devices: 21 us -> none  [copy_for_each(): return lax.all_to_all(copies, axis, split_axis=0, concat_axis=0, tiled=True)]
    all_to_all x4 -> x0, waiting for transfers between devices: 15.2 us -> none  [copy_for_each(): return lax.all_to_all(copies, axis, split_axis=0, concat_axis=0, tiled=True)]
    slice x15 -> x0, local copies, waits for them, and re-layouts: 14.4 us -> none  [the longest x1 8.01 us: level_two_conv(): stacked[:, z_tap:z_tap + out_depth, y_tap * row_len:y_tap * row_len + fla...]
    all_gather x2 -> x0, blocking collectives: 13.6 us -> none  [the longest x1 7.28 us: per_device(): lax.all_gather(edged, SY, axis=0, tiled=True)]
  transfers between devices with their start and end apart: 16 -> 0, of which waited for: 9 -> 0; matrix products, arithmetic and copies ran while one was open for 6% -> 0% of each run, Pallas kernels for 0% -> 0%
where the time goes in v1:
time: 57.5 us; the launch traced here: 57.3 us
  Pallas kernels  52.9 us (92%)
  local copies, waits for them, and re-layouts  3.72 us (6%)
  between operations  0.65 us (1%)
    pallas_call x1, Pallas kernels, step(): pl.pallas_call(functools.partial(body_entry, ny, nz, gx, gy), out_shape=(...  52.9 us
    unnamed x4, local copies, waits for them, and re-layouts  3.21 us

profile of v1, /device:TPU:1, one launch (start us, length us, event | category | flops | bytes accessed | tf_op | source)
XLA Modules:
  0.0 57.3 jit_solution(8379612073425495907)
XLA Ops:
  0.6 52.9 %encoder.1 = (bf16[32,4,8,128]{3,2,1,0:T(8,128)(2,1)}, bf16[2,16,1024]{2,1,0:T(8,128)(2,1)}, f32[1,128]{1,0:T(1,128)}) custom-call(bf16[32,4,8,128]{3,2,1,0:T(8,128)(2,1)} %bitcast.11, f32[4,16]{1,0:T(4,128)} %refs_1_.1, bf16[9,96,32]{2,1,0:T(8,128)(2,1)} %bitcast.13, bf16[9,96,32]{2,1,0:T(8,128)(2,1)} %bitcast.14, bf16[9,48,32]{2,1,0:T(8,128)(2,1)} %bitcast.15, ...), custom_call_target="tpu_custom_call" | custom-call | tf_op jit(solution)/shard_map/encoder/pallas_call | solution.py:565
  53.6 0.0 copy-start
  53.6 1.5 %copy.13 = bf16[1,16,2,1024]{3,2,1,0:T(2,128)(2,1)} copy(bf16[1,16,2,1024]{3,1,2,0:T(8,128)(2,1)} %bitcast.17) | data formatting | bytes 131072
  55.1 0.0 copy-done
  55.1 0.5 slice_bitcast_fusion
  55.6 1.7 %copy.15 = bf16[1,32,4,8,128]{4,3,2,1,0:T(8,128)(2,1)} copy(bf16[1,32,4,8,128]{4,3,2,1,0:T(8,128)(2,1)} %bitcast.12) | data formatting | bytes 524288
Async XLA Ops:
  53.6 1.6 %copy-start = (f32[1,128]{1,0:T(1,128)S(1)}, f32[1,128]{1,0:T(1,128)}, u32[]{:S(2)}) copy-start(f32[1,128]{1,0:T(1,128)} %get-tuple-element.8) | copy-start | bytes 1540

commit v2 on v1

--- a/solution.py
+++ b/solution.py
@@ -17,10 +17,10 @@
 
 def body(
     ny, nz, gx, gy,
-    vol, hist, w1, w2, w3, w4, gf, sf, gc, sc,
+    vol, hist_h, w1, w2, w3, w4, gf_h, sf_h, gc_h, sc_h,
     skip, coarse, amax,
-    vin, w1v, w2v, w3v, w4v, wf1, wf2, wg3, wg4,
-    x1, r1, x2r, x2, r2, h3, p3, c3, h4, r4i, c4, a2a, a2s, gcol,
+    hist, gf, sf, gc, sc, vin, w1v, w2v, w3v, w4v, wf1, wf2, wg3, wg4,
+    x1, r1, x2r, x2, r2, h3, z3s, z3r, p3, c3, c3z, h4, z4s, z4r, r4i, c4, c4z, a2a, a2s, gcol,
     st, am, outv, rows8,
     lsem, osem, hs, hr, ss, sr, ws, wr, gs, gr, bs, br, xs, xr,
 ):
@@ -32,10 +32,11 @@
     mx_, my_ = lax.rem(smp, gx), lax.div(smp, gx)
 
     loads = [pltpu.make_async_copy(vol.at[:, z], vin.at[z], lsem.at[z]) for z in range(4)]
-    for i, (s, d) in enumerate(((w1, w1v), (w2, w2v), (w3, w3v), (w4, w4v))):
+    small = ((hist_h, hist), (w1, w1v), (w2, w2v), (w3, w3v), (w4, w4v), (gf_h, gf), (sf_h, sf), (gc_h, gc), (sc_h, sc))
+    for i, (s, d) in enumerate(small):
         loads.append(pltpu.make_async_copy(s, d, lsem.at[4 + i]))
-    for c in loads:
-        c.start()
+    for i in (4, 0, 3, 1, 2, 5, 6, 7, 8, 9, 10, 11, 12):
+        loads[i].start()
 
     def partner(d):
         p = lax.rem(me + d, n)
@@ -69,6 +70,7 @@
         return cond
 
     lane = lax.broadcasted_iota(jnp.int32, (1, 128), 1)
+    lower = lane < 64
 
     def bound_of(l):
         b = jnp.max(hist[l : l + 1, :], axis=1, keepdims=True)
@@ -109,6 +111,64 @@
             def _():
                 halo(ph, buf, zl, yl, i).wait_send()
 
+    def coarse_halo(ph, own, zs, zr, i):
+        dz, dy = DIRS[i]
+        if dz == 0:
+            src, dst = own.at[src_z(dy, 4)], own.at[dst_z(dy, 4)]
+        else:
+            up = 1 if dz > 0 else 0
+            src, dst = zs.at[up, src_z(dy, 4)], zr.at[1 - up, dst_z(dy, 4)]
+        return pltpu.make_async_remote_copy(
+            src_ref=src, dst_ref=dst, send_sem=hs.at[ph, i], recv_sem=hr.at[ph, i],
+            device_id={"sy": sy + dy, "sz": sz + dz}, device_id_type=MESH,
+        )
+
+    def coarse_send(ph, own, zs, zr):
+        for i in range(8):
+            @pl.when(exists(*DIRS[i]))
+            def _():
+                coarse_halo(ph, own, zs, zr, i).start()
+
+    def coarse_done(ph, own, zs, zr):
+        for i in range(8):
+            @pl.when(exists(*DIRS[i]))
+            def _():
+                coarse_halo(ph, own, zs, zr, i).wait_send()
+
+    def put_raw(blk, y, own, zs):
+        half = blk.shape[0] // 2
+        top, low = blk[:half], blk[half:]
+        own[y] = blk.astype(BF16)
+        zs[0, y] = jnp.where(lower, top, pltpu.roll(low, 64, 1)).astype(BF16)
+        zs[1, y] = jnp.where(lower, pltpu.roll(top, 64, 1), low).astype(BF16)
+
+    def coarse_settle(ph, own, zs, zr, buf, zbuf, aff, b):
+        half = buf.shape[1] // 2
+        paff = tuple(jnp.where(lower, t[:half], t[half:]) for t in aff)
+        for i in range(8):
+            dz, dy = DIRS[i]
+            there = exists(-dz, -dy)
+            ys = slots(dy, 4)
+
+            @pl.when(there)
+            def _():
+                coarse_halo(ph, own, zs, zr, i).wait_recv()
+                for y in ys:
+                    if dz == 0:
+                        buf[y] = settle(own[y].astype(F32), aff, b)
+                    else:
+                        k = 0 if dz > 0 else 1
+                        zbuf[k, y] = settle(zr[k, y].astype(F32), paff, b)
+
+            @pl.when(jnp.logical_not(there))
+            def _():
+                for y in ys:
+                    if dz == 0:
+                        buf[y] = jnp.zeros(buf.shape[1:], BF16)
+                    else:
+                        k = 0 if dz > 0 else 1
+                        zbuf[k, y] = jnp.zeros(zbuf.shape[2:], BF16)
+
     def slots(d, length):
         return range(1, length + 1) if d == 0 else ((0,) if d > 0 else (length + 1,))
 
@@ -150,16 +210,6 @@
         t = (v - m) * a + s
         return jnp.maximum(t, SLOPE * t)
 
-    rows8[...] = jnp.zeros_like(rows8)
-    rows8[0:2, 0:32] = gf[...]
-    rows8[2:4, 0:32] = sf[...]
-    rows8[4:6, 0:16] = gc[...]
-    rows8[6:8, 0:16] = sc[...]
-    gcols = jnp.transpose(rows8[...])
-
-    def gain_col(j, count):
-        return jnp.broadcast_to(gcols[0:count, j : j + 1], (count, 128))
-
     ri = lax.broadcasted_iota(jnp.int32, (256, 256), 0)
     ci = lax.broadcasted_iota(jnp.int32, (256, 256), 1)
 
@@ -168,13 +218,13 @@
 
     into = onehot(jnp.logical_and((ri & 31) == (ci >> 3), (ri >> 5) == (ci & 7)))
 
+    loads[4].wait()
     b0 = bound_of(0)
-    for i in range(4):
-        loads[i].wait()
     peak0 = jnp.zeros((256, 128), F32)
-    for zp in range(2):
+    for zp in ((0, 3), (1, 2)):
         parts = []
-        for z in (2 * zp, 2 * zp + 1):
+        for z in zp:
+            loads[z].wait()
             v = vin[z].astype(F32).reshape(256, 128)
             peak0 = jnp.maximum(peak0, jnp.abs(v))
             parts.append(v.astype(BF16))
@@ -182,14 +232,24 @@
         moved = jnp.clip(moved, -b0, b0).astype(BF16)
         for k in range(2):
             for y in range(8):
-                x1[1 + 2 * zp + k, 1 + y] = moved[32 * y : 32 * y + 32, 128 * k : 128 * k + 128]
+                x1[1 + zp[k], 1 + y] = moved[32 * y : 32 * y + 32, 128 * k : 128 * k + 128]
     peak0 = jnp.max(jnp.max(peak0, axis=0, keepdims=True), axis=1, keepdims=True)
 
     pl.semaphore_wait(barrier, (n - 1) + (gx - 1) + (gy - 1))
     halo_send(0, x1, 4, 8, range(8))
 
-    for i in range(4, 8):
+    for i in range(5, 13):
         loads[i].wait()
+    rows8[...] = jnp.zeros_like(rows8)
+    rows8[0:2, 0:32] = gf[...]
+    rows8[2:4, 0:32] = sf[...]
+    rows8[4:6, 0:16] = gc[...]
+    rows8[6:8, 0:16] = sc[...]
+    gcols = jnp.transpose(rows8[...])
+
+    def gain_col(j, count):
+        return jnp.broadcast_to(gcols[0:count, j : j + 1], (count, 128))
+
 
     def lanes_of(w):
         return jnp.concatenate([w[k] for k in range(9)], axis=1)
@@ -274,10 +334,38 @@
         for y in range(8):
             r1[z, y] = outs[y]
             x2r[z + 1, y + 1] = outs[y].astype(BF16)
-        halo_send(1, x2r, 4, 8, (0, 2, 3) if z == 0 else (1, 4, 5))
-    halo_send(1, x2r, 4, 8, (6, 7))
     row = mixed_row(jnp.concatenate(acc, axis=0))
     stat_send(0, jnp.concatenate([row, jnp.broadcast_to(peak0, (1, 128))], axis=0))
+    halo_send(1, x2r, 4, 8, range(8))
+
+    mate = sy + 1 - 2 * lax.rem(sy, 2)
+    cross_sy = lax.rem(sy + 2, 4)
+    cross_mate = lax.rem(mate + 2, 4)
+
+    def group(which, kind, src):
+        buf = (wg3, wg4, gcol)[which]
+        return pltpu.make_async_remote_copy(
+            src_ref=buf.at[src], dst_ref=buf.at[src],
+            send_sem=ws.at[which, kind], recv_sem=wr.at[which, src],
+            device_id={"sy": cross_sy if kind == 1 else mate}, device_id_type=MESH,
+        )
+
+    for which in (2, 0, 1):
+        group(which, 1, sy).start()
+        group(which, 0, sy).start()
+
+    def group_forward(which):
+        group(which, 1, cross_sy).wait_recv()
+        group(which, 2, cross_sy).start()
+
+    def group_wait(which):
+        group(which, 0, mate).wait_recv()
+        group(which, 2, cross_mate).wait_recv()
+
+    def group_done(which):
+        group(which, 0, sy).wait_send()
+        group(which, 1, sy).wait_send()
+        group(which, 2, cross_sy).wait_send()
 
     fine_cells = float(4 * nz * 8 * ny * 128)
     coarse_cells = fine_cells / 8
@@ -331,18 +419,8 @@
             r2[z, y] = outs[y]
     settle_halo(1, x2r, x2, 4, 8, range(6), aff, b1)
 
-    def group(d, src, which):
-        q = lax.rem(sy + d, ny)
-        buf = (wg3, wg4, gcol)[which]
-        return pltpu.make_async_remote_copy(
-            src_ref=buf.at[sy], dst_ref=buf.at[src],
-            send_sem=ws.at[which, d], recv_sem=wr.at[which, src],
-            device_id={"sy": q}, device_id_type=MESH,
-        )
-
-    for which in range(3):
-        for d in range(1, ny):
-            group(d, sy, which).start()
+    for which in (2, 0, 1):
+        group_forward(which)
 
     for z in (0, 3):
         outs = fine_conv(x2, wb, z)
@@ -374,12 +452,12 @@
     for yp in range(4):
         blk = pooled[32 * yp : 32 * yp + 32]
         p3[yp] = blk
-        h3[1, yp + 1] = blk.astype(BF16)
+        put_raw(blk, yp + 1, h3, z3s)
         hi = jnp.maximum(hi, blk)
         lo = jnp.minimum(lo, blk)
-    halo_send(2, h3, 1, 4, range(8))
     row = mixed_row(jnp.concatenate([acc[0], acc[1], hi, lo], axis=0))
     stat_send(1, jnp.concatenate([row, row], axis=0))
+    coarse_send(2, h3, z3s, z3r)
 
     got = stat_wait(1)
     cols = mixed_total(got)
@@ -387,22 +465,26 @@
     peak2 = peak_of(cols[64:96], cols[96:128], aff2)
     b2 = bound_of(2)
     for yp in range(4):
-        c3[1, yp + 1] = settle(p3[yp], aff2, b2)
-    settle_halo(2, h3, c3, 1, 4, range(8), aff2, b2)
-
-    lower = lane < 64
+        c3[yp + 1] = settle(p3[yp], aff2, b2)
+    coarse_settle(2, h3, z3s, z3r, c3, c3z, aff2, b2)
+
     cfirst, clast = (lane & 63) == 0, (lane & 63) == 63
 
-    def coarse_conv(buf, w):
+    def coarse_conv(buf, zbuf, w):
         strips = []
-        mids = [buf[1, y] for y in range(6)]
+        mids = [buf[y] for y in range(6)]
         pairs = [[], mids, []]
+        half = buf.shape[1] // 2
         for y in range(6):
-            own = mids[y].astype(F32)
-            prev = buf[0, y].astype(F32)
-            nxt = buf[2, y].astype(F32)
-            pairs[0].append(pltpu.roll(jnp.where(lower, own, prev), 64, 1).astype(BF16))
-            pairs[2].append(pltpu.roll(jnp.where(lower, nxt, own), 64, 1).astype(BF16))
+            own = pltpu.roll(mids[y].astype(F32), 64, 1)
+            prev = zbuf[0, y].astype(F32)
+            nxt = zbuf[1, y].astype(F32)
+            a = jnp.where(lower, prev, own[:half])
+            b = jnp.where(lower, pltpu.roll(prev, 64, 1), own[half:])
+            pairs[0].append(jnp.concatenate([a, b], axis=0).astype(BF16))
+            a = jnp.where(lower, own[:half], pltpu.roll(nxt, 64, 1))
+            b = jnp.where(lower, own[half:], nxt)
+            pairs[2].append(jnp.concatenate([a, b], axis=0).astype(BF16))
         for zt in range(3):
             for yt in range(3):
                 strips.append(jnp.concatenate(pairs[zt][yt : yt + 4], axis=1))
@@ -417,16 +499,14 @@
             outs.append(jnp.concatenate(parts, axis=0))
         return outs
 
-    for d in range(1, ny):
-        group(d, lax.rem(sy + d, ny), 0).wait_recv()
-    outs = coarse_conv(c3, wg3[...].reshape(192, 288))
+    group_wait(0)
+    outs = coarse_conv(c3, c3z, wg3[...].reshape(192, 288))
     zero64 = jnp.zeros((64, 128), F32)
     acc = (zero64, zero64, jnp.full((64, 128), -jnp.inf, F32), jnp.full((64, 128), jnp.inf, F32))
     acc = gather_stats(acc, outs, True)
     for y in range(4):
-        h4[1, y + 1] = outs[y].astype(BF16)
+        put_raw(outs[y], y + 1, h4, z4s)
         r4i[y] = outs[y]
-    halo_send(3, h4, 1, 4, range(8))
 
     def double_rows(acc, extremes):
         t = to_rows(jnp.concatenate(acc[0:2], axis=0))
@@ -439,6 +519,7 @@
         return jnp.concatenate([r0, jnp.where(lower, high, low)], axis=0)
 
     stat_send(2, double_rows(acc, True))
+    coarse_send(3, h4, z4s, z4r)
 
     outof = onehot(jnp.logical_and((ci & 31) == (ri >> 3), (ci >> 5) == (ri & 7)))
     stores = []
@@ -453,8 +534,7 @@
             stores.append(pltpu.make_async_copy(outv.at[z], skip.at[:, z], osem.at[z]))
             stores[-1].start()
 
-    for d in range(1, ny):
-        group(d, lax.rem(sy + d, ny), 2).wait_recv()
+    group_wait(2)
     gall = gcol[...]
     got = stat_wait(2)
     cols = to_cols(jnp.sum(got[:, 0:1, :], axis=0))
@@ -480,12 +560,11 @@
         cross(0, d, mx_).start()
 
     for y in range(4):
-        c4[1, y + 1] = settle(r4i[y], aff3, b3)
-    settle_halo(3, h4, c4, 1, 4, range(8), aff3, b3)
-
-    for d in range(1, ny):
-        group(d, lax.rem(sy + d, ny), 1).wait_recv()
-    outs = coarse_conv(c4, wg4[...].reshape(192, 576))
+        c4[y + 1] = settle(r4i[y], aff3, b3)
+    coarse_settle(3, h4, z4s, z4r, c4, c4z, aff3, b3)
+
+    group_wait(1)
+    outs = coarse_conv(c4, c4z, wg4[...].reshape(192, 576))
     acc = gather_stats((zero64, zero64, None, None), outs, False)
     for g in range(4):
         for y in range(4):
@@ -499,9 +578,9 @@
             device_id={"sy": q}, device_id_type=MESH,
         )
 
+    stat_send(3, double_rows(acc, False))
     for d in range(1, ny):
         swap(d, sy).start()
-    stat_send(3, double_rows(acc, False))
     a2a[sy] = a2s[sy]
 
     for d in range(1, gx):
@@ -536,14 +615,13 @@
         c.wait()
     halo_done(0, x1, 4, 8)
     halo_done(1, x2r, 4, 8)
-    halo_done(2, h3, 1, 4)
-    halo_done(3, h4, 1, 4)
+    coarse_done(2, h3, z3s, z3r)
+    coarse_done(3, h4, z4s, z4r)
     for ph in range(4):
         for d in order:
             stat_copy(ph, d, me).wait_send()
     for which in range(3):
-        for d in range(1, ny):
-            group(d, sy, which).wait_send()
+        group_done(which)
     for d in range(1, ny):
         swap(d, sy).wait_send()
     for d in range(1, gx):
@@ -569,9 +647,14 @@
                 jax.ShapeDtypeStruct((2, 16, 1024), BF16),
                 jax.ShapeDtypeStruct((1, 128), F32),
             ),
-            in_specs=[hbm, vmem, hbm, hbm, hbm, hbm, vmem, vmem, vmem, vmem],
+            in_specs=[hbm] * 10,
             out_specs=(hbm, vmem, vmem),
             scratch_shapes=[
+                pltpu.VMEM((4, 16), F32),
+                pltpu.VMEM((2, 32), F32),
+                pltpu.VMEM((2, 32), F32),
+                pltpu.VMEM((2, 16), F32),
+                pltpu.VMEM((2, 16), F32),
                 pltpu.VMEM((4, 32, 8, 128), BF16),
                 pltpu.VMEM((9, 96, 32), BF16),
                 pltpu.VMEM((9, 96, 32), BF16),
@@ -586,12 +669,18 @@
                 pltpu.VMEM((6, 10, 32, 128), BF16),
                 pltpu.VMEM((6, 10, 32, 128), BF16),
                 pltpu.VMEM((4, 8, 32, 128), F32),
-                pltpu.VMEM((3, 6, 32, 128), BF16),
+                pltpu.VMEM((6, 32, 128), BF16),
+                pltpu.VMEM((2, 6, 16, 128), BF16),
+                pltpu.VMEM((2, 6, 16, 128), BF16),
                 pltpu.VMEM((4, 32, 128), F32),
-                pltpu.VMEM((3, 6, 32, 128), BF16),
-                pltpu.VMEM((3, 6, 64, 128), BF16),
+                pltpu.VMEM((6, 32, 128), BF16),
+                pltpu.VMEM((2, 6, 16, 128), BF16),
+                pltpu.VMEM((6, 64, 128), BF16),
+                pltpu.VMEM((2, 6, 32, 128), BF16),
+                pltpu.VMEM((2, 6, 32, 128), BF16),
                 pltpu.VMEM((4, 64, 128), F32),
-                pltpu.VMEM((3, 6, 64, 128), BF16),
+                pltpu.VMEM((6, 64, 128), BF16),
+                pltpu.VMEM((2, 6, 32, 128), BF16),
                 pltpu.VMEM((ny, 4, 16, 128), F32),
                 pltpu.VMEM((ny, 4, 16, 128), F32),
                 pltpu.VMEM((ny, 2, 16, 128), F32),
@@ -600,13 +689,13 @@
                 pltpu.VMEM((4, 32, 8, 128), BF16),
                 pltpu.VMEM((8, 128), F32),
                 pltpu.VMEM((128, 128), F32),
-                dma((8,)),
+                dma((13,)),
                 dma((4,)),
                 dma((4, 8)),
                 dma((4, 8)),
                 dma((4, n)),
                 dma((4, n)),
-                dma((3, ny)),
+                dma((3, 3)),
                 dma((3, ny)),
                 dma((ny,)),
                 dma((ny,)),
@@ -640,16 +729,16 @@
 def body_entry(ny, nz, gx, gy, *refs):
     (
         vol, hist, w1, w2, w3, w4, gf, sf, gc, sc, skip, coarse, amax,
-        vin, w1v, w2v, w3v, w4v, wf1, wf2, wg3, wg4,
-        x1, r1, x2r, x2, r2, h3, p3, c3, h4, r4i, c4, a2a, a2s, gcol,
+        hist_v, gf_v, sf_v, gc_v, sc_v, vin, w1v, w2v, w3v, w4v, wf1, wf2, wg3, wg4,
+        x1, r1, x2r, x2, r2, h3, z3s, z3r, p3, c3, c3z, h4, z4s, z4r, r4i, c4, c4z, a2a, a2s, gcol,
         st, am, outv, rows8, tcols,
         lsem, osem, hs, hr, ss, sr, ws, wr, bs, br, xs, xr,
     ) = refs
     body(
         ny, nz, gx, gy,
         vol, hist, w1, w2, w3, w4, gf, sf, gc, sc, skip, coarse, amax,
-        vin, w1v, w2v, w3v, w4v, wf1, wf2, wg3, wg4,
-        x1, r1, x2r, x2, r2, h3, p3, c3, h4, r4i, c4, a2a, a2s, gcol,
+        hist_v, gf_v, sf_v, gc_v, sc_v, vin, w1v, w2v, w3v, w4v, wf1, wf2, wg3, wg4,
+        x1, r1, x2r, x2, r2, h3, z3s, z3r, p3, c3, c3z, h4, z4s, z4r, r4i, c4, c4z, a2a, a2s, gcol,
         st, am, outv, rows8,
         lsem, osem, hs, hr, ss, sr, ws, wr, tcols, None, bs, br, xs, xr,
     )

time: 57.5 us -> 48.7 us (0.85)
  Pallas kernels: 52.9 us -> 44 us
    pallas_call x1, Pallas kernels: 52.9 us -> 44 us  [step(): pl.pallas_call(functools.partial(body_entry, ny, nz, gx, gy), out_shape=(...]
where the time goes in v2:
time: 48.7 us; the launch traced here: 48.4 us
  Pallas kernels  44 us (90%)
  local copies, waits for them, and re-layouts  3.72 us (8%)
  between operations  0.65 us (1%)
    pallas_call x1, Pallas kernels, step(): pl.pallas_call(functools.partial(body_entry, ny, nz, gx, gy), out_shape=(...  44 us
    unnamed x4, local copies, waits for them, and re-layouts  3.21 us

profile of v2, /device:TPU:1, one launch (start us, length us, event | category | flops | bytes accessed | tf_op | source)
XLA Modules:
  0.0 48.4 jit_solution(10833862688202984702)
XLA Ops:
  0.6 44.0 %encoder.1 = (bf16[32,4,8,128]{3,2,1,0:T(8,128)(2,1)}, bf16[2,16,1024]{2,1,0:T(8,128)(2,1)}, f32[1,128]{1,0:T(1,128)}) custom-call(bf16[32,4,8,128]{3,2,1,0:T(8,128)(2,1)} %bitcast.11, f32[4,16]{1,0:T(4,128)} %refs_1_.1, bf16[9,96,32]{2,1,0:T(8,128)(2,1)} %bitcast.13, bf16[9,96,32]{2,1,0:T(8,128)(2,1)} %bitcast.14, bf16[9,48,32]{2,1,0:T(8,128)(2,1)} %bitcast.15, ...), custom_call_target="tpu_custom_call" | custom-call | tf_op jit(solution)/shard_map/encoder/pallas_call | solution.py:643
  44.6 0.0 copy-start
  44.6 1.5 %copy.13 = bf16[1,16,2,1024]{3,2,1,0:T(2,128)(2,1)} copy(bf16[1,16,2,1024]{3,1,2,0:T(8,128)(2,1)} %bitcast.17) | data formatting | bytes 131072
  46.2 0.0 copy-done
  46.2 0.5 %slice_bitcast_fusion = f32[4]{0:T(128)} fusion(f32[1,128]{1,0:T(1,128)S(1)} %copy-done), kind=kLoop, calls=%fused_computation | loop fusion | bytes 32 | tf_op jit(solution)/shard_map/squeeze | solution.py:714
  46.7 1.7 %copy.15 = bf16[1,32,4,8,128]{4,3,2,1,0:T(8,128)(2,1)} copy(bf16[1,32,4,8,128]{4,3,2,1,0:T(8,128)(2,1)} %bitcast.12) | data formatting | bytes 524288
Async XLA Ops:
  44.6 1.6 %copy-start = (f32[1,128]{1,0:T(1,128)S(1)}, f32[1,128]{1,0:T(1,128)}, u32[]{:S(2)}) copy-start(f32[1,128]{1,0:T(1,128)} %get-tuple-element.8) | copy-start | bytes 1540

commit v3 on v2

--- a/solution.py
+++ b/solution.py
@@ -16,20 +16,36 @@
 
 
 def body(
-    ny, nz, gx, gy,
+    ny, nz, ns,
     vol, hist_h, w1, w2, w3, w4, gf_h, sf_h, gc_h, sc_h,
     skip, coarse, amax,
     hist, gf, sf, gc, sc, vin, w1v, w2v, w3v, w4v, wf1, wf2, wg3, wg4,
     x1, r1, x2r, x2, r2, h3, z3s, z3r, p3, c3, c3z, h4, z4s, z4r, r4i, c4, c4z, a2a, a2s, gcol,
-    st, am, outv, rows8,
-    lsem, osem, hs, hr, ss, sr, ws, wr, gs, gr, bs, br, xs, xr,
+    st, am, rows8,
+    rounds, lsem, hs, hr, ss, sr, ws, wr, gs, gr, bs, br, xs, xr,
 ):
     n = ny * nz
     sy = lax.axis_index("sy")
     sz = lax.axis_index("sz")
     smp = lax.axis_index("sample")
     me = sz * ny + sy
-    mx_, my_ = lax.rem(smp, gx), lax.div(smp, gx)
+
+    near = [{"sz": lax.rem(sz + d, nz)} for d in sorted({1, nz - 1})]
+    near += [{"sy": lax.rem(sy + d, ny)} for d in range(1, ny)]
+    if ns > 1:
+        sx, sv = lax.rem(smp, 4), lax.div(smp, 4)
+        near += [{"sample": sv * 4 + lax.rem(sx + d, 4)} for d in (1, 3)]
+        near += [{"sample": lax.rem(sv + d, 4) * 4 + sx} for d in (1, 3)]
+    barrier = pltpu.get_barrier_semaphore()
+    for dev in near:
+        pl.semaphore_signal(barrier, inc=1, device_id=dev, device_id_type=MESH)
+
+    def greet(r):
+        for dev in near:
+            pl.semaphore_signal(rounds.at[r], inc=1, device_id=dev, device_id_type=MESH)
+
+    def greeted(r):
+        pl.semaphore_wait(rounds.at[r], len(near))
 
     loads = [pltpu.make_async_copy(vol.at[:, z], vin.at[z], lsem.at[z]) for z in range(4)]
     small = ((hist_h, hist), (w1, w1v), (w2, w2v), (w3, w3v), (w4, w4v), (gf_h, gf), (sf_h, sf), (gc_h, gc), (sc_h, sc))
@@ -43,22 +59,9 @@
         return p, {"sy": lax.rem(p, ny), "sz": lax.div(p, ny)}
 
     order = sorted(range(1, n), key=lambda d: -min(d, n - d))
-    barrier = pltpu.get_barrier_semaphore()
-    for d in order:
-        pl.semaphore_signal(barrier, inc=1, device_id=partner(d)[1], device_id_type=MESH)
-
-    def xpeer(d):
-        q = lax.rem(mx_ + d, gx)
-        return q, {"sample": my_ * gx + q}
-
-    def ypeer(d):
-        q = lax.rem(my_ + d, gy)
-        return q, {"sample": q * gx + mx_}
-
-    for d in range(1, gx):
-        pl.semaphore_signal(barrier, inc=1, device_id=xpeer(d)[1], device_id_type=MESH)
-    for d in range(1, gy):
-        pl.semaphore_signal(barrier, inc=1, device_id=ypeer(d)[1], device_id_type=MESH)
+    def other_sample(d):
+        q = lax.rem(smp + d, ns)
+        return q, {"sample": q}
 
     def exists(dz, dy):
         cond = None
@@ -235,8 +238,9 @@
                 x1[1 + zp[k], 1 + y] = moved[32 * y : 32 * y + 32, 128 * k : 128 * k + 128]
     peak0 = jnp.max(jnp.max(peak0, axis=0, keepdims=True), axis=1, keepdims=True)
 
-    pl.semaphore_wait(barrier, (n - 1) + (gx - 1) + (gy - 1))
-    halo_send(0, x1, 4, 8, range(8))
+    pl.semaphore_wait(barrier, len(near))
+    greet(0)
+    halo_send(0, x1, 4, 8, (0, 1, 6, 7))
 
     for i in range(5, 13):
         loads[i].wait()
@@ -271,6 +275,9 @@
                         buf[z, y] = jnp.zeros(buf.shape[2:], buf.dtype)
 
     zero_missing(x1, 4, 8)
+    greeted(0)
+    greet(1)
+    halo_send(0, x1, 4, 8, (2, 3, 4, 5))
 
     first, last = lane == 0, lane == 127
 
@@ -335,6 +342,8 @@
             r1[z, y] = outs[y]
             x2r[z + 1, y + 1] = outs[y].astype(BF16)
     row = mixed_row(jnp.concatenate(acc, axis=0))
+    greeted(1)
+    greet(2)
     stat_send(0, jnp.concatenate([row, jnp.broadcast_to(peak0, (1, 128))], axis=0))
     halo_send(1, x2r, 4, 8, range(8))
 
@@ -418,9 +427,6 @@
         for y in range(8):
             r2[z, y] = outs[y]
     settle_halo(1, x2r, x2, 4, 8, range(6), aff, b1)
-
-    for which in (2, 0, 1):
-        group_forward(which)
 
     for z in (0, 3):
         outs = fine_conv(x2, wb, z)
@@ -458,6 +464,8 @@
     row = mixed_row(jnp.concatenate([acc[0], acc[1], hi, lo], axis=0))
     stat_send(1, jnp.concatenate([row, row], axis=0))
     coarse_send(2, h3, z3s, z3r)
+    for which in (2, 0, 1):
+        group_forward(which)
 
     got = stat_wait(1)
     cols = mixed_total(got)
@@ -522,7 +530,6 @@
     coarse_send(3, h4, z4s, z4r)
 
     outof = onehot(jnp.logical_and((ci & 31) == (ri >> 3), (ci >> 5) == (ri & 7)))
-    stores = []
     for zp in range(2):
         parts = []
         for z in (2 * zp, 2 * zp + 1):
@@ -530,9 +537,7 @@
         moved = jnp.dot(outof, jnp.concatenate(parts, axis=1), preferred_element_type=F32)
         for k in range(2):
             z = 2 * zp + k
-            outv[z] = moved[:, 128 * k : 128 * k + 128].reshape(32, 8, 128).astype(BF16)
-            stores.append(pltpu.make_async_copy(outv.at[z], skip.at[:, z], osem.at[z]))
-            stores[-1].start()
+            skip[z] = moved[:, 128 * k : 128 * k + 128].reshape(32, 8, 128).astype(BF16)
 
     group_wait(2)
     gall = gcol[...]
@@ -547,17 +552,17 @@
 
     peaks = jnp.where(lane == 0, peak0, jnp.where(lane == 1, peak1, jnp.where(lane == 2, peak2, peak3)))
 
-    def cross(step, d, src):
-        mine, peer = (mx_, xpeer) if step == 0 else (my_, ypeer)
+    def cross(d, src):
         return pltpu.make_async_remote_copy(
-            src_ref=am.at[step, mine], dst_ref=am.at[step, src],
-            send_sem=xs.at[step, d], recv_sem=xr.at[step, src],
-            device_id=peer(d)[1], device_id_type=MESH,
+            src_ref=am.at[smp], dst_ref=am.at[src],
+            send_sem=xs.at[d], recv_sem=xr.at[src],
+            device_id=other_sample(d)[1], device_id_type=MESH,
         )
 
-    am[0, mx_] = peaks
-    for d in range(1, gx):
-        cross(0, d, mx_).start()
+    greeted(2)
+    am[smp] = peaks
+    for d in range(1, ns):
+        cross(d, smp).start()
 
     for y in range(4):
         c4[y + 1] = settle(r4i[y], aff3, b3)
@@ -582,12 +587,6 @@
     for d in range(1, ny):
         swap(d, sy).start()
     a2a[sy] = a2s[sy]
-
-    for d in range(1, gx):
-        cross(0, d, xpeer(d)[0]).wait_recv()
-    am[1, my_] = jnp.max(am[0, 0:gx], axis=0)
-    for d in range(1, gy):
-        cross(1, d, my_).start()
 
     for d in range(1, ny):
         swap(d, lax.rem(sy + d, ny)).wait_recv()
@@ -607,12 +606,10 @@
     for z in range(2):
         coarse[z] = jnp.concatenate(planes[z], axis=1).astype(BF16)
 
-    for d in range(1, gy):
-        cross(1, d, ypeer(d)[0]).wait_recv()
-    amax[...] = jnp.max(am[1, 0:gy], axis=0)
-
-    for c in stores:
-        c.wait()
+    for d in range(1, ns):
+        cross(d, other_sample(d)[0]).wait_recv()
+    amax[...] = jnp.max(am[...], axis=0)
+
     halo_done(0, x1, 4, 8)
     halo_done(1, x2r, 4, 8)
     coarse_done(2, h3, z3s, z3r)
@@ -624,16 +621,12 @@
         group_done(which)
     for d in range(1, ny):
         swap(d, sy).wait_send()
-    for d in range(1, gx):
-        cross(0, d, mx_).wait_send()
-    for d in range(1, gy):
-        cross(1, d, my_).wait_send()
+    for d in range(1, ns):
+        cross(d, smp).wait_send()
 
 
 def solution(mesh):
     ny, nz, ns = mesh.shape["sy"], mesh.shape["sz"], mesh.shape["sample"]
-    gx = 4 if ns % 4 == 0 else ns
-    gy = ns // gx
     n = ny * nz
     vmem = pl.BlockSpec(memory_space=pltpu.VMEM)
     hbm = pl.BlockSpec(memory_space=pl.ANY)
@@ -641,14 +634,14 @@
     def step(volume, hist, w1, w2, w3, w4, gf, sf, gc, sc):
         dma = pltpu.SemaphoreType.DMA
         skip, coarse, amax = pl.pallas_call(
-            functools.partial(body_entry, ny, nz, gx, gy),
+            functools.partial(body_entry, ny, nz, ns),
             out_shape=(
-                jax.ShapeDtypeStruct((32, 4, 8, 128), BF16),
-                jax.ShapeDtypeStruct((2, 16, 1024), BF16),
-                jax.ShapeDtypeStruct((1, 128), F32),
+                pltpu.VMEM((4, 32, 8, 128), BF16),
+                pltpu.VMEM((2, 16, 1024), BF16),
+                pltpu.VMEM((1, 128), F32),
             ),
             in_specs=[hbm] * 10,
-            out_specs=(hbm, vmem, vmem),
+            out_specs=(vmem, vmem, vmem),
             scratch_shapes=[
                 pltpu.VMEM((4, 16), F32),
                 pltpu.VMEM((2, 32), F32),
@@ -685,12 +678,11 @@
                 pltpu.VMEM((ny, 4, 16, 128), F32),
                 pltpu.VMEM((ny, 2, 16, 128), F32),
                 pltpu.VMEM((4, n, 2, 128), F32),
-                pltpu.VMEM((2, 4, 1, 128), F32),
-                pltpu.VMEM((4, 32, 8, 128), BF16),
+                pltpu.VMEM((ns, 1, 128), F32),
                 pltpu.VMEM((8, 128), F32),
                 pltpu.VMEM((128, 128), F32),
+                pltpu.SemaphoreType.REGULAR((3,)),
                 dma((13,)),
-                dma((4,)),
                 dma((4, 8)),
                 dma((4, 8)),
                 dma((4, n)),
@@ -699,8 +691,8 @@
                 dma((3, ny)),
                 dma((ny,)),
                 dma((ny,)),
-                dma((2, 4)),
-                dma((2, 4)),
+                dma((ns,)),
+                dma((ns,)),
             ],
             compiler_params=pltpu.CompilerParams(collective_id=0, has_side_effects=True),
             name="encoder",
@@ -708,11 +700,19 @@
             volume.reshape(32, 4, 8, 128), hist, w1.reshape(9, 96, 32), w2.reshape(9, 96, 32),
             w3.reshape(9, 48, 32), w4.reshape(9, 48, 64), gf, sf, gc, sc,
         )
-        return (
-            skip.reshape(1, 32, 4, 8, 128),
-            jnp.transpose(coarse, (1, 0, 2)).reshape(1, 16, 2, 1024),
-            amax[0, :4],
-        )
+        skip, coarse, amax = pl.pallas_call(
+            emit,
+            out_shape=(
+                jax.ShapeDtypeStruct((32, 4, 8, 128), BF16),
+                jax.ShapeDtypeStruct((16, 2, 1024), BF16),
+                jax.ShapeDtypeStruct((1, 4), F32),
+            ),
+            in_specs=[vmem] * 3,
+            out_specs=(hbm, vmem, vmem),
+            scratch_shapes=[dma((4,))],
+            name="emit",
+        )(*(pltpu.with_memory_space_constraint(t, pltpu.VMEM) for t in (skip, coarse, amax)))
+        return skip.reshape(1, 32, 4, 8, 128), coarse.reshape(1, 16, 2, 1024), amax.reshape(4)
 
     return jax.shard_map(
         step,
@@ -726,19 +726,29 @@
     )
 
 
-def body_entry(ny, nz, gx, gy, *refs):
+def body_entry(ny, nz, ns, *refs):
     (
         vol, hist, w1, w2, w3, w4, gf, sf, gc, sc, skip, coarse, amax,
         hist_v, gf_v, sf_v, gc_v, sc_v, vin, w1v, w2v, w3v, w4v, wf1, wf2, wg3, wg4,
         x1, r1, x2r, x2, r2, h3, z3s, z3r, p3, c3, c3z, h4, z4s, z4r, r4i, c4, c4z, a2a, a2s, gcol,
-        st, am, outv, rows8, tcols,
-        lsem, osem, hs, hr, ss, sr, ws, wr, bs, br, xs, xr,
+        st, am, rows8, tcols,
+        rounds, lsem, hs, hr, ss, sr, ws, wr, bs, br, xs, xr,
     ) = refs
     body(
-        ny, nz, gx, gy,
+        ny, nz, ns,
         vol, hist, w1, w2, w3, w4, gf, sf, gc, sc, skip, coarse, amax,
         hist_v, gf_v, sf_v, gc_v, sc_v, vin, w1v, w2v, w3v, w4v, wf1, wf2, wg3, wg4,
         x1, r1, x2r, x2, r2, h3, z3s, z3r, p3, c3, c3z, h4, z4s, z4r, r4i, c4, c4z, a2a, a2s, gcol,
-        st, am, outv, rows8,
-        lsem, osem, hs, hr, ss, sr, ws, wr, tcols, None, bs, br, xs, xr,
+        st, am, rows8,
+        rounds, lsem, hs, hr, ss, sr, ws, wr, tcols, None, bs, br, xs, xr,
     )
+
+
+def emit(skip_v, coarse_v, amax_v, skip, coarse, amax, sem):
+    copies = [pltpu.make_async_copy(skip_v.at[z], skip.at[:, z], sem.at[z]) for z in range(4)]
+    for c in copies:
+        c.start()
+    coarse[...] = jnp.stack([coarse_v[0].astype(F32), coarse_v[1].astype(F32)], axis=1).astype(BF16)
+    amax[...] = amax_v[0:1, 0:4]
+    for c in copies:
+        c.wait()

time: 48.7 us -> 43.6 us (0.90)
  local copies, waits for them, and re-layouts: 3.72 us -> 0 us
  Pallas kernels: 44 us -> 42.8 us
    unnamed x4 -> x0, local copies, waits for them, and re-layouts: 3.21 us -> none
    pallas_call x1 -> x2, Pallas kernels: 44 us -> 42.8 us  [the longest x1 41.5 us: step(): pl.pallas_call(functools.partial(body_entry, ny, nz, ns), out_shape=(pltp...]
    squeeze x1 -> x0, local copies, waits for them, and re-layouts: 0.51 us -> none  [step(): amax[0, :4]]
where the time goes in v3:
time: 43.6 us; the launch traced here: 43.5 us
  Pallas kernels  42.8 us (98%)
  between operations  0.64 us (1%)
    pallas_call x1, Pallas kernels, step(): pl.pallas_call(functools.partial(body_entry, ny, nz, ns), out_shape=(pltp...  41.5 us
    pallas_call x1, Pallas kernels, step(): pl.pallas_call(emit, out_shape=(jax.ShapeDtypeStruct((32, 4, 8, 128), BF1...  1.36 us

profile of v3, /device:TPU:1, one launch (start us, length us, event | category | flops | bytes accessed | tf_op | source)
XLA Modules:
  0.0 43.5 jit_solution(12288440077995690749)
XLA Ops:
  0.6 41.5 %encoder.1 = (bf16[4,32,8,128]{3,2,1,0:T(8,128)(2,1)S(1)}, bf16[2,16,1024]{2,1,0:T(8,128)(2,1)S(1)}, f32[1,128]{1,0:T(1,128)S(1)}) custom-call(bf16[32,4,8,128]{3,2,1,0:T(8,128)(2,1)} %bitcast.8, f32[4,16]{1,0:T(4,128)} %refs_1_.1, bf16[9,96,32]{2,1,0:T(8,128)(2,1)} %bitcast.9, bf16[9,96,32]{2,1,0:T(8,128)(2,1)} %bitcast.10, bf16[9,48,32]{2,1,0:T(8,128)(2,1)} %bitcast.11, ...), custom_call_target="tpu_custom_call" | custom-call | tf_op jit(solution)/shard_map/encoder/pallas_call | solution.py:636
  42.1 1.4 %emit.1 = (bf16[32,4,8,128]{3,2,1,0:T(8,128)(2,1)}, bf16[16,2,1024]{2,1,0:T(2,128)(2,1)}, f32[1,4]{1,0:T(1,128)}) custom-call(bf16[4,32,8,128]{3,2,1,0:T(8,128)(2,1)S(1)} %get-tuple-element.9.skip_v, bf16[2,16,1024]{2,1,0:T(8,128)(2,1)S(1)} %get-tuple-element.10.coarse_v, f32[1,128]{1,0:T(1,128)S(1)} %get-tuple-element.11.amax_v), custom_call_target="tpu_custom_call" | custom-call | tf_op jit(solution)/shard_map/emit/pallas_call | solution.py:703

commit v4 on v3

--- a/solution.py
+++ b/solution.py
@@ -20,7 +20,7 @@
     vol, hist_h, w1, w2, w3, w4, gf_h, sf_h, gc_h, sc_h,
     skip, coarse, amax,
     hist, gf, sf, gc, sc, vin, w1v, w2v, w3v, w4v, wf1, wf2, wg3, wg4,
-    x1, r1, x2r, x2, r2, h3, z3s, z3r, p3, c3, c3z, h4, z4s, z4r, r4i, c4, c4z, a2a, a2s, gcol,
+    x1, r1, x2r, x2, r2, h3, z3s, z3r, p3, c3, c3z, h4, z4s, z4r, r4i, c4, c4z, a2a, a2s, grow,
     st, am, rows8,
     rounds, lsem, hs, hr, ss, sr, ws, wr, gs, gr, bs, br, xs, xr,
 ):
@@ -187,7 +187,7 @@
         )
 
     def stat_send(ph, rows):
-        st[ph, me] = rows
+        st[ph, me] = jnp.concatenate(rows + [rows[0]] * (4 - len(rows)), axis=0)
         for d in order:
             stat_copy(ph, d, me).start()
 
@@ -223,24 +223,29 @@
 
     loads[4].wait()
     b0 = bound_of(0)
-    peak0 = jnp.zeros((256, 128), F32)
-    for zp in ((0, 3), (1, 2)):
+    peaks0 = []
+
+    def take(zp):
         parts = []
         for z in zp:
             loads[z].wait()
             v = vin[z].astype(F32).reshape(256, 128)
-            peak0 = jnp.maximum(peak0, jnp.abs(v))
+            peaks0.append(jnp.abs(v))
             parts.append(v.astype(BF16))
         moved = jnp.dot(into, jnp.concatenate(parts, axis=1), preferred_element_type=F32)
         moved = jnp.clip(moved, -b0, b0).astype(BF16)
         for k in range(2):
             for y in range(8):
                 x1[1 + zp[k], 1 + y] = moved[32 * y : 32 * y + 32, 128 * k : 128 * k + 128]
-    peak0 = jnp.max(jnp.max(peak0, axis=0, keepdims=True), axis=1, keepdims=True)
-
+
+    take((0, 3))
     pl.semaphore_wait(barrier, len(near))
     greet(0)
-    halo_send(0, x1, 4, 8, (0, 1, 6, 7))
+    halo_send(0, x1, 4, 8, (0, 1))
+    take((1, 2))
+    halo_send(0, x1, 4, 8, (6, 7))
+    peak0 = jnp.maximum(jnp.maximum(peaks0[0], peaks0[1]), jnp.maximum(peaks0[2], peaks0[3]))
+    peak0 = jnp.max(jnp.max(peak0, axis=0, keepdims=True), axis=1, keepdims=True)
 
     for i in range(5, 13):
         loads[i].wait()
@@ -262,8 +267,8 @@
     wf2[...] = lanes_of(w2v)
     wg3[sy] = lanes_of(w3v)
     wg4[sy] = lanes_of(w4v)
-    gcol[sy, 0] = gain_col(4, 16)
-    gcol[sy, 1] = gain_col(6, 16)
+    grow[sy, 0] = rows8[4]
+    grow[sy, 1] = rows8[6]
 
     def zero_missing(buf, zl, yl):
         for i in range(8):
@@ -275,9 +280,50 @@
                         buf[z, y] = jnp.zeros(buf.shape[2:], buf.dtype)
 
     zero_missing(x1, 4, 8)
+    mate = sy + 1 - 2 * lax.rem(sy, 2)
+    cross_sy = lax.rem(sy + 2, 4)
+    cross_mate = lax.rem(mate + 2, 4)
+
+    def group(which, kind, src):
+        buf = (wg3, wg4, grow)[which]
+        return pltpu.make_async_remote_copy(
+            src_ref=buf.at[src], dst_ref=buf.at[src],
+            send_sem=ws.at[which, kind], recv_sem=wr.at[which, src],
+            device_id={"sy": cross_sy if kind == 1 else mate}, device_id_type=MESH,
+        )
+
+    def group_send(which):
+        group(which, 1, sy).start()
+        group(which, 0, sy).start()
+
+    def group_forward(which):
+        group(which, 1, cross_sy).wait_recv()
+        group(which, 2, cross_sy).start()
+
+    def group_wait(which):
+        group(which, 0, mate).wait_recv()
+        group(which, 2, cross_mate).wait_recv()
+
+    def group_done(which):
+        group(which, 0, sy).wait_send()
+        group(which, 1, sy).wait_send()
+        group(which, 2, cross_sy).wait_send()
+
+    fine_cells = float(4 * nz * 8 * ny * 128)
+    coarse_cells = fine_cells / 8
+
+    def fine_affine(cols, j):
+        return affine(cols[0:32], cols[32:64], fine_cells, gain_col(j, 32), gain_col(2 + j, 32))
+
+    def peak_of(high, low, aff):
+        v = jnp.maximum(jnp.abs(act(high, aff)), jnp.abs(act(low, aff))).astype(BF16).astype(F32)
+        return jnp.max(jnp.max(v, axis=0, keepdims=True), axis=1, keepdims=True)
+
     greeted(0)
     greet(1)
     halo_send(0, x1, 4, 8, (2, 3, 4, 5))
+    group_send(2)
+    group_send(0)
 
     first, last = lane == 0, lane == 127
 
@@ -310,6 +356,12 @@
                 hi = jnp.maximum(hi, b)
                 lo = jnp.minimum(lo, b)
         return s, q, hi, lo
+
+    def sum_row(cols):
+        cols = jnp.concatenate(cols, axis=0)
+        if cols.shape[0] < 128:
+            cols = jnp.concatenate([cols, cols], axis=0)
+        return jnp.sum(to_rows(cols), axis=0, keepdims=True)
 
     def mixed_row(cols):
         t = to_rows(cols)
@@ -344,47 +396,10 @@
     row = mixed_row(jnp.concatenate(acc, axis=0))
     greeted(1)
     greet(2)
-    stat_send(0, jnp.concatenate([row, jnp.broadcast_to(peak0, (1, 128))], axis=0))
+    stat_send(0, [row, jnp.broadcast_to(peak0, (1, 128))])
     halo_send(1, x2r, 4, 8, range(8))
-
-    mate = sy + 1 - 2 * lax.rem(sy, 2)
-    cross_sy = lax.rem(sy + 2, 4)
-    cross_mate = lax.rem(mate + 2, 4)
-
-    def group(which, kind, src):
-        buf = (wg3, wg4, gcol)[which]
-        return pltpu.make_async_remote_copy(
-            src_ref=buf.at[src], dst_ref=buf.at[src],
-            send_sem=ws.at[which, kind], recv_sem=wr.at[which, src],
-            device_id={"sy": cross_sy if kind == 1 else mate}, device_id_type=MESH,
-        )
-
-    for which in (2, 0, 1):
-        group(which, 1, sy).start()
-        group(which, 0, sy).start()
-
-    def group_forward(which):
-        group(which, 1, cross_sy).wait_recv()
-        group(which, 2, cross_sy).start()
-
-    def group_wait(which):
-        group(which, 0, mate).wait_recv()
-        group(which, 2, cross_mate).wait_recv()
-
-    def group_done(which):
-        group(which, 0, sy).wait_send()
-        group(which, 1, sy).wait_send()
-        group(which, 2, cross_sy).wait_send()
-
-    fine_cells = float(4 * nz * 8 * ny * 128)
-    coarse_cells = fine_cells / 8
-
-    def fine_affine(cols, j):
-        return affine(cols[0:32], cols[32:64], fine_cells, gain_col(j, 32), gain_col(2 + j, 32))
-
-    def peak_of(high, low, aff):
-        v = jnp.maximum(jnp.abs(act(high, aff)), jnp.abs(act(low, aff))).astype(BF16).astype(F32)
-        return jnp.max(jnp.max(v, axis=0, keepdims=True), axis=1, keepdims=True)
+    group_forward(2)
+    group_forward(0)
 
     got = stat_wait(0)
     peak0 = jnp.max(jnp.max(got[:, 1:2, :], axis=0), axis=1, keepdims=True)
@@ -434,6 +449,7 @@
         for y in range(8):
             r2[z, y] = outs[y]
 
+    stat_send(1, [sum_row(acc[0:2])])
     s_r = lax.broadcasted_iota(jnp.int32, (256, 128), 0)
     s_c = lax.broadcasted_iota(jnp.int32, (256, 128), 1)
     pick = onehot(s_r == jnp.where(s_c < 64, 2 * s_c, 2 * s_c))
@@ -461,16 +477,12 @@
         put_raw(blk, yp + 1, h3, z3s)
         hi = jnp.maximum(hi, blk)
         lo = jnp.minimum(lo, blk)
-    row = mixed_row(jnp.concatenate([acc[0], acc[1], hi, lo], axis=0))
-    stat_send(1, jnp.concatenate([row, row], axis=0))
     coarse_send(2, h3, z3s, z3r)
-    for which in (2, 0, 1):
-        group_forward(which)
+    group_send(1)
 
     got = stat_wait(1)
-    cols = mixed_total(got)
+    cols = to_cols(jnp.sum(got[:, 0:1, :], axis=0))
     aff2 = fine_affine(cols, 1)
-    peak2 = peak_of(cols[64:96], cols[96:128], aff2)
     b2 = bound_of(2)
     for yp in range(4):
         c3[yp + 1] = settle(p3[yp], aff2, b2)
@@ -512,22 +524,17 @@
     zero64 = jnp.zeros((64, 128), F32)
     acc = (zero64, zero64, jnp.full((64, 128), -jnp.inf, F32), jnp.full((64, 128), jnp.inf, F32))
     acc = gather_stats(acc, outs, True)
+
+    def extreme_row(cols, split):
+        t = to_rows(jnp.concatenate(cols, axis=0))
+        return jnp.where(split, jnp.max(t, axis=0, keepdims=True), jnp.min(t, axis=0, keepdims=True))
+
+    stat_send(2, [sum_row(acc[0:2]), extreme_row(acc[2:4], lower), extreme_row((hi, hi, lo, lo), lower)])
     for y in range(4):
         put_raw(outs[y], y + 1, h4, z4s)
         r4i[y] = outs[y]
-
-    def double_rows(acc, extremes):
-        t = to_rows(jnp.concatenate(acc[0:2], axis=0))
-        r0 = jnp.sum(t, axis=0, keepdims=True)
-        if not extremes:
-            return jnp.concatenate([r0, r0], axis=0)
-        t = to_rows(jnp.concatenate(acc[2:4], axis=0))
-        high = jnp.max(t, axis=0, keepdims=True)
-        low = jnp.min(t, axis=0, keepdims=True)
-        return jnp.concatenate([r0, jnp.where(lower, high, low)], axis=0)
-
-    stat_send(2, double_rows(acc, True))
     coarse_send(3, h4, z4s, z4r)
+    group_forward(1)
 
     outof = onehot(jnp.logical_and((ci & 31) == (ri >> 3), (ci >> 5) == (ri & 7)))
     for zp in range(2):
@@ -540,13 +547,20 @@
             skip[z] = moved[:, 128 * k : 128 * k + 128].reshape(32, 8, 128).astype(BF16)
 
     group_wait(2)
-    gall = gcol[...]
+    gall = jnp.transpose(grow[...].reshape(2 * ny, 128))
+
+    def gathered(k):
+        parts = [gall[0:16, 2 * g + k : 2 * g + k + 1] for g in range(ny)]
+        return jnp.broadcast_to(jnp.concatenate(parts, axis=0), (64, 128))
+
     got = stat_wait(2)
     cols = to_cols(jnp.sum(got[:, 0:1, :], axis=0))
-    high = jnp.max(got[:, 1:2, :], axis=0)
-    low = jnp.min(got[:, 1:2, :], axis=0)
-    ext = to_cols(jnp.where(lower, high, low))
-    aff3 = affine(cols[0:64], cols[64:128], coarse_cells, gall[:, 0].reshape(64, 128), gall[:, 1].reshape(64, 128))
+    high = jnp.max(got[:, 1:3, :], axis=0)
+    low = jnp.min(got[:, 1:3, :], axis=0)
+    ext = jnp.where(lower, high, low)
+    pext, ext = to_cols(ext[1:2]), to_cols(ext[0:1])
+    peak2 = peak_of(pext[0:32], pext[64:96], aff2)
+    aff3 = affine(cols[0:64], cols[64:128], coarse_cells, gathered(0), gathered(1))
     peak3 = peak_of(ext[0:64], ext[64:128], aff3)
     b3 = bound_of(3)
 
@@ -559,22 +573,18 @@
             device_id=other_sample(d)[1], device_id_type=MESH,
         )
 
+    for y in range(4):
+        c4[y + 1] = settle(r4i[y], aff3, b3)
+    coarse_settle(3, h4, z4s, z4r, c4, c4z, aff3, b3)
     greeted(2)
     am[smp] = peaks
     for d in range(1, ns):
         cross(d, smp).start()
 
-    for y in range(4):
-        c4[y + 1] = settle(r4i[y], aff3, b3)
-    coarse_settle(3, h4, z4s, z4r, c4, c4z, aff3, b3)
 
     group_wait(1)
     outs = coarse_conv(c4, c4z, wg4[...].reshape(192, 576))
     acc = gather_stats((zero64, zero64, None, None), outs, False)
-    for g in range(4):
-        for y in range(4):
-            a2s[g, y] = outs[y][16 * g : 16 * g + 16]
-
     def swap(d, src):
         q = lax.rem(sy + d, ny)
         return pltpu.make_async_remote_copy(
@@ -583,11 +593,24 @@
             device_id={"sy": q}, device_id_type=MESH,
         )
 
-    stat_send(3, double_rows(acc, False))
+    stat_send(3, [sum_row(acc[0:2])])
+    for g in range(4):
+        for y in range(4):
+            a2s[g, y] = outs[y][16 * g : 16 * g + 16]
+
     for d in range(1, ny):
         swap(d, sy).start()
     a2a[sy] = a2s[sy]
 
+    halo_done(0, x1, 4, 8)
+    halo_done(1, x2r, 4, 8)
+    coarse_done(2, h3, z3s, z3r)
+    coarse_done(3, h4, z4s, z4r)
+    for ph in range(3):
+        for d in order:
+            stat_copy(ph, d, me).wait_send()
+    for which in range(3):
+        group_done(which)
     for d in range(1, ny):
         swap(d, lax.rem(sy + d, ny)).wait_recv()
     got = stat_wait(3)
@@ -603,22 +626,15 @@
             v = act(a2a[g, 2 * yp + 1], aff4)
             planes[0].append(jnp.where(lower, u, pltpu.roll(v, 64, 1)))
             planes[1].append(jnp.where(lower, pltpu.roll(u, 64, 1), v))
-    for z in range(2):
-        coarse[z] = jnp.concatenate(planes[z], axis=1).astype(BF16)
+    both = [jnp.concatenate(planes[z], axis=1) for z in range(2)]
+    coarse[...] = jnp.stack(both, axis=1).astype(BF16)
 
     for d in range(1, ns):
         cross(d, other_sample(d)[0]).wait_recv()
-    amax[...] = jnp.max(am[...], axis=0)
-
-    halo_done(0, x1, 4, 8)
-    halo_done(1, x2r, 4, 8)
-    coarse_done(2, h3, z3s, z3r)
-    coarse_done(3, h4, z4s, z4r)
-    for ph in range(4):
-        for d in order:
-            stat_copy(ph, d, me).wait_send()
-    for which in range(3):
-        group_done(which)
+    amax[...] = jnp.max(am[...], axis=0)[:, 0:4]
+
+    for d in order:
+        stat_copy(3, d, me).wait_send()
     for d in range(1, ny):
         swap(d, sy).wait_send()
     for d in range(1, ns):
@@ -637,8 +653,8 @@
             functools.partial(body_entry, ny, nz, ns),
             out_shape=(
                 pltpu.VMEM((4, 32, 8, 128), BF16),
-                pltpu.VMEM((2, 16, 1024), BF16),
-                pltpu.VMEM((1, 128), F32),
+                pltpu.VMEM((16, 2, 1024), BF16),
+                pltpu.VMEM((1, 4), F32),
             ),
             in_specs=[hbm] * 10,
             out_specs=(vmem, vmem, vmem),
@@ -676,8 +692,8 @@
                 pltpu.VMEM((2, 6, 32, 128), BF16),
                 pltpu.VMEM((ny, 4, 16, 128), F32),
                 pltpu.VMEM((ny, 4, 16, 128), F32),
-                pltpu.VMEM((ny, 2, 16, 128), F32),
-                pltpu.VMEM((4, n, 2, 128), F32),
+                pltpu.VMEM((ny, 2, 128), F32),
+                pltpu.VMEM((4, n, 4, 128), F32),
                 pltpu.VMEM((ns, 1, 128), F32),
                 pltpu.VMEM((8, 128), F32),
                 pltpu.VMEM((128, 128), F32),
@@ -708,8 +724,8 @@
                 jax.ShapeDtypeStruct((1, 4), F32),
             ),
             in_specs=[vmem] * 3,
-            out_specs=(hbm, vmem, vmem),
-            scratch_shapes=[dma((4,))],
+            out_specs=(hbm, hbm, hbm),
+            scratch_shapes=[dma((6,))],
             name="emit",
         )(*(pltpu.with_memory_space_constraint(t, pltpu.VMEM) for t in (skip, coarse, amax)))
         return skip.reshape(1, 32, 4, 8, 128), coarse.reshape(1, 16, 2, 1024), amax.reshape(4)
@@ -730,7 +746,7 @@
     (
         vol, hist, w1, w2, w3, w4, gf, sf, gc, sc, skip, coarse, amax,
         hist_v, gf_v, sf_v, gc_v, sc_v, vin, w1v, w2v, w3v, w4v, wf1, wf2, wg3, wg4,
-        x1, r1, x2r, x2, r2, h3, z3s, z3r, p3, c3, c3z, h4, z4s, z4r, r4i, c4, c4z, a2a, a2s, gcol,
+        x1, r1, x2r, x2, r2, h3, z3s, z3r, p3, c3, c3z, h4, z4s, z4r, r4i, c4, c4z, a2a, a2s, grow,
         st, am, rows8, tcols,
         rounds, lsem, hs, hr, ss, sr, ws, wr, bs, br, xs, xr,
     ) = refs
@@ -738,7 +754,7 @@
         ny, nz, ns,
         vol, hist, w1, w2, w3, w4, gf, sf, gc, sc, skip, coarse, amax,
         hist_v, gf_v, sf_v, gc_v, sc_v, vin, w1v, w2v, w3v, w4v, wf1, wf2, wg3, wg4,
-        x1, r1, x2r, x2, r2, h3, z3s, z3r, p3, c3, c3z, h4, z4s, z4r, r4i, c4, c4z, a2a, a2s, gcol,
+        x1, r1, x2r, x2, r2, h3, z3s, z3r, p3, c3, c3z, h4, z4s, z4r, r4i, c4, c4z, a2a, a2s, grow,
         st, am, rows8,
         rounds, lsem, hs, hr, ss, sr, ws, wr, tcols, None, bs, br, xs, xr,
     )
@@ -746,9 +762,9 @@
 
 def emit(skip_v, coarse_v, amax_v, skip, coarse, amax, sem):
     copies = [pltpu.make_async_copy(skip_v.at[z], skip.at[:, z], sem.at[z]) for z in range(4)]
+    copies.append(pltpu.make_async_copy(coarse_v, coarse, sem.at[4]))
+    copies.append(pltpu.make_async_copy(amax_v, amax, sem.at[5]))
     for c in copies:
         c.start()
-    coarse[...] = jnp.stack([coarse_v[0].astype(F32), coarse_v[1].astype(F32)], axis=1).astype(BF16)
-    amax[...] = amax_v[0:1, 0:4]
     for c in copies:
         c.wait()

time: 43.6 us -> 42.8 us (0.982)
  Pallas kernels: 42.8 us -> 42 us
    pallas_call x1, Pallas kernels: 1.36 us -> 0.77 us  [step(): pl.pallas_call(emit, out_shape=(jax.ShapeDtypeStruct((32, 4, 8, 128), BF1...]
where the time goes in v4:
time: 42.8 us; the launch traced here: 42.7 us
  Pallas kernels  42 us (98%)
  between operations  0.64 us (1%)
    pallas_call x1, Pallas kernels, step(): pl.pallas_call(functools.partial(body_entry, ny, nz, ns), out_shape=(pltp...  41.3 us

profile of v4, /device:TPU:1, one launch (start us, length us, event | category | flops | bytes accessed | tf_op | source)
XLA Modules:
  0.0 42.7 jit_solution(6188821571614539284)
XLA Ops:
  0.6 41.3 %encoder.1 = (bf16[4,32,8,128]{3,2,1,0:T(8,128)(2,1)S(1)}, bf16[16,2,1024]{2,1,0:T(2,128)(2,1)S(1)}, f32[1,4]{1,0:T(1,128)S(1)}) custom-call(bf16[32,4,8,128]{3,2,1,0:T(8,128)(2,1)} %bitcast.8, f32[4,16]{1,0:T(4,128)} %refs_1_.1, bf16[9,96,32]{2,1,0:T(8,128)(2,1)} %bitcast.9, bf16[9,96,32]{2,1,0:T(8,128)(2,1)} %bitcast.10, bf16[9,48,32]{2,1,0:T(8,128)(2,1)} %bitcast.11, ...), custom_call_target="tpu_custom_call" | custom-call | tf_op jit(solution)/shard_map/encoder/pallas_call | solution.py:652
  41.9 0.8 %emit.1 = (bf16[32,4,8,128]{3,2,1,0:T(8,128)(2,1)}, bf16[16,2,1024]{2,1,0:T(2,128)(2,1)}, f32[1,4]{1,0:T(1,128)}) custom-call(bf16[4,32,8,128]{3,2,1,0:T(8,128)(2,1)S(1)} %get-tuple-element.9.skip_v, bf16[16,2,1024]{2,1,0:T(2,128)(2,1)S(1)} %get-tuple-element.10.coarse_v, f32[1,4]{1,0:T(1,128)S(1)} %get-tuple-element.11.amax_v), custom_call_target="tpu_custom_call" | custom-call | tf_op jit(solution)/shard_map/emit/pallas_call | solution.py:719

commit v5 on v4

--- a/solution.py
+++ b/solution.py
@@ -12,6 +12,12 @@
 BF16 = jnp.bfloat16
 EPS = 1e-05
 SLOPE = 0.01
+PIECES = (
+    ((-1, 0, 1, 6), (1, 0, 1, 6), (-1, 0, 7, 2), (1, 0, 7, 2), (-1, -1, 1, 1), (-1, 1, 8, 1), (1, -1, 1, 1), (1, 1, 8, 1),
+     (0, -1, 1, 1), (0, 1, 8, 1)),
+    ((-1, 0, 2, 4), (1, 0, 2, 4), (-1, 0, 6, 3), (1, 0, 6, 3), (-1, -1, 1, 1), (-1, 1, 8, 1), (1, -1, 1, 1), (1, 1, 8, 1),
+     (0, -1, 1, 1), (0, 1, 8, 1), (-1, 0, 1, 1), (1, 0, 1, 1)),
+)
 DIRS = ((-1, 0), (1, 0), (-1, -1), (-1, 1), (1, -1), (1, 1), (0, -1), (0, 1))
 
 
@@ -22,7 +28,7 @@
     hist, gf, sf, gc, sc, vin, w1v, w2v, w3v, w4v, wf1, wf2, wg3, wg4,
     x1, r1, x2r, x2, r2, h3, z3s, z3r, p3, c3, c3z, h4, z4s, z4r, r4i, c4, c4z, a2a, a2s, grow,
     st, am, rows8,
-    rounds, lsem, hs, hr, ss, sr, ws, wr, gs, gr, bs, br, xs, xr,
+    rounds, lsem, hs, hr, ss, sr, ws, wr, gs, bs, xs,
 ):
     n = ny * nz
     sy = lax.axis_index("sy")
@@ -85,34 +91,38 @@
     def dst_z(dz, zl):
         return pl.ds(1, zl) if dz == 0 else (pl.ds(zl + 1, 1) if dz < 0 else pl.ds(0, 1))
 
-    def halo(ph, buf, zl, yl, i):
-        dz, dy = DIRS[i]
+    def halo(ph, buf, i):
+        dz, dy, row, count = PIECES[ph][i]
         return pltpu.make_async_remote_copy(
-            src_ref=buf.at[src_z(dz, zl), src_z(dy, yl)],
-            dst_ref=buf.at[dst_z(dz, zl), dst_z(dy, yl)],
-            send_sem=hs.at[ph, i],
-            recv_sem=hr.at[ph, i],
+            src_ref=buf.at[src_z(dz, 4), pl.ds(row, count)],
+            dst_ref=buf.at[dst_z(dz, 4), pl.ds(row - 8 * dy, count)],
+            send_sem=hs.at[ph % 2, i],
+            recv_sem=hr.at[ph % 2, i],
             device_id={"sy": sy + dy, "sz": sz + dz},
             device_id_type=MESH,
         )
 
-    def halo_send(ph, buf, zl, yl, which):
+    def halo_send(ph, buf, which):
         for i in which:
-            @pl.when(exists(*DIRS[i]))
-            def _():
-                halo(ph, buf, zl, yl, i).start()
-
-    def halo_wait(ph, buf, zl, yl, which):
+            @pl.when(exists(*PIECES[ph][i][:2]))
+            def _():
+                halo(ph, buf, i).start()
+
+    def halo_wait(ph, buf, which):
         for i in which:
-            @pl.when(exists(-DIRS[i][0], -DIRS[i][1]))
-            def _():
-                halo(ph, buf, zl, yl, i).wait_recv()
-
-    def halo_done(ph, buf, zl, yl):
-        for i in range(8):
-            @pl.when(exists(*DIRS[i]))
-            def _():
-                halo(ph, buf, zl, yl, i).wait_send()
+            @pl.when(exists(-PIECES[ph][i][0], -PIECES[ph][i][1]))
+            def _():
+                halo(ph, buf, i).wait_recv()
+
+    def halo_done(ph, buf):
+        for i in range(len(PIECES[ph])):
+            @pl.when(exists(*PIECES[ph][i][:2]))
+            def _():
+                halo(ph, buf, i).wait_send()
+
+    def halo_slots(ph, i):
+        dz, dy, row, count = PIECES[ph][i]
+        return slots(dz, 4), range(row - 8 * dy, row - 8 * dy + count)
 
     def coarse_halo(ph, own, zs, zr, i):
         dz, dy = DIRS[i]
@@ -122,7 +132,7 @@
             up = 1 if dz > 0 else 0
             src, dst = zs.at[up, src_z(dy, 4)], zr.at[1 - up, dst_z(dy, 4)]
         return pltpu.make_async_remote_copy(
-            src_ref=src, dst_ref=dst, send_sem=hs.at[ph, i], recv_sem=hr.at[ph, i],
+            src_ref=src, dst_ref=dst, send_sem=hs.at[ph % 2, i], recv_sem=hr.at[ph % 2, i],
             device_id={"sy": sy + dy, "sz": sz + dz}, device_id_type=MESH,
         )
 
@@ -175,25 +185,24 @@
     def slots(d, length):
         return range(1, length + 1) if d == 0 else ((0,) if d > 0 else (length + 1,))
 
-    def stat_copy(ph, d, src):
-        p, dev = partner(d)
+    def stat_copy(ph, src, dst, dev):
         return pltpu.make_async_remote_copy(
-            src_ref=st.at[ph, me],
-            dst_ref=st.at[ph, src],
-            send_sem=ss.at[ph, d],
-            recv_sem=sr.at[ph, src],
-            device_id=dev,
-            device_id_type=MESH,
+            src_ref=st.at[ph, src], dst_ref=st.at[ph, dst],
+            send_sem=ss.at[ph], recv_sem=sr.at[ph],
+            device_id=dev, device_id_type=MESH,
         )
+
+    def stat_all(ph):
+        rest = pl.ds(0, n - 1)
+        return stat_copy(ph, rest, rest, partner(1)[1])
 
     def stat_send(ph, rows):
         st[ph, me] = jnp.concatenate(rows + [rows[0]] * (4 - len(rows)), axis=0)
         for d in order:
-            stat_copy(ph, d, me).start()
+            stat_copy(ph, me, me, partner(d)[1]).start()
 
     def stat_wait(ph):
-        for d in order:
-            stat_copy(ph, d, partner(d)[0]).wait_recv()
+        stat_all(ph).wait_recv()
         return st[ph]
 
     def to_rows(cols):
@@ -241,9 +250,9 @@
     take((0, 3))
     pl.semaphore_wait(barrier, len(near))
     greet(0)
-    halo_send(0, x1, 4, 8, (0, 1))
+    halo_send(0, x1, (0, 1))
     take((1, 2))
-    halo_send(0, x1, 4, 8, (6, 7))
+    halo_send(0, x1, (8, 9, 2, 3))
     peak0 = jnp.maximum(jnp.maximum(peaks0[0], peaks0[1]), jnp.maximum(peaks0[2], peaks0[3]))
     peak0 = jnp.max(jnp.max(peak0, axis=0, keepdims=True), axis=1, keepdims=True)
 
@@ -270,16 +279,13 @@
     grow[sy, 0] = rows8[4]
     grow[sy, 1] = rows8[6]
 
-    def zero_missing(buf, zl, yl):
-        for i in range(8):
-            dz, dy = DIRS[i]
-            @pl.when(jnp.logical_not(exists(-dz, -dy)))
-            def _():
-                for z in slots(dz, zl):
-                    for y in slots(dy, yl):
-                        buf[z, y] = jnp.zeros(buf.shape[2:], buf.dtype)
-
-    zero_missing(x1, 4, 8)
+    for i in range(len(PIECES[0])):
+        @pl.when(jnp.logical_not(exists(-PIECES[0][i][0], -PIECES[0][i][1])))
+        def _():
+            for z in halo_slots(0, i)[0]:
+                for y in halo_slots(0, i)[1]:
+                    x1[z, y] = jnp.zeros((32, 128), BF16)
+
     mate = sy + 1 - 2 * lax.rem(sy, 2)
     cross_sy = lax.rem(sy + 2, 4)
     cross_mate = lax.rem(mate + 2, 4)
@@ -321,9 +327,7 @@
 
     greeted(0)
     greet(1)
-    halo_send(0, x1, 4, 8, (2, 3, 4, 5))
-    group_send(2)
-    group_send(0)
+    halo_send(0, x1, (4, 5, 6, 7))
 
     first, last = lane == 0, lane == 127
 
@@ -332,16 +336,15 @@
         right = jnp.where(hi, 0.0, pltpu.roll(p2, 127, 1))
         return p1 + left + right
 
-    def fine_conv(buf, w, z):
+    def fine_conv(buf, w, z, rows=range(8)):
         strips = []
         for zt in range(3):
-            blocks = [buf[z + zt, y] for y in range(10)]
             for yt in range(3):
-                strips.append(jnp.concatenate(blocks[yt : yt + 8], axis=1))
+                strips.append(jnp.concatenate([buf[z + zt, y + yt] for y in rows], axis=1))
         got = jnp.dot(w, jnp.concatenate(strips, axis=0), preferred_element_type=F32)
         outs = []
-        for y in range(8):
-            blk = got[:, 128 * y : 128 * y + 128]
+        for k in range(len(rows)):
+            blk = got[:, 128 * k : 128 * k + 128]
             outs.append(combine(blk[0:32], blk[32:64], blk[64:96], first, last))
         return outs
 
@@ -378,28 +381,31 @@
 
     wa = wf1[...]
     acc = (zero, zero, jnp.full((32, 128), -jnp.inf, F32), jnp.full((32, 128), jnp.inf, F32))
-    halo_wait(0, x1, 4, 8, (6, 7))
+    def first_rows(z, rows, acc):
+        outs = fine_conv(x1, wa, z, rows)
+        for k, y in enumerate(rows):
+            r1[z, y] = outs[k]
+            if z in (0, 3) or y in (0, 7):
+                x2r[z + 1, y + 1] = outs[k].astype(BF16)
+        return gather_stats(acc, outs, True)
+
+    halo_wait(0, x1, (0, 1))
+    for z in (0, 3):
+        acc = first_rows(z, (1, 2, 3, 4), acc)
+    halo_send(1, x2r, (0, 1))
+    halo_wait(0, x1, (8, 9))
     for z in (1, 2):
-        outs = fine_conv(x1, wa, z)
-        acc = gather_stats(acc, outs, True)
-        for y in range(8):
-            r1[z, y] = outs[y]
-        x2r[z + 1, 1] = outs[0].astype(BF16)
-        x2r[z + 1, 8] = outs[7].astype(BF16)
-    halo_wait(0, x1, 4, 8, range(6))
+        acc = first_rows(z, range(8), acc)
+    halo_wait(0, x1, range(2, 8))
     for z in (0, 3):
-        outs = fine_conv(x1, wa, z)
-        acc = gather_stats(acc, outs, True)
-        for y in range(8):
-            r1[z, y] = outs[y]
-            x2r[z + 1, y + 1] = outs[y].astype(BF16)
+        acc = first_rows(z, (0, 5, 6, 7), acc)
     row = mixed_row(jnp.concatenate(acc, axis=0))
     greeted(1)
     greet(2)
     stat_send(0, [row, jnp.broadcast_to(peak0, (1, 128))])
-    halo_send(1, x2r, 4, 8, range(8))
-    group_forward(2)
-    group_forward(0)
+    halo_send(1, x2r, (2, 3, 10, 11, 4, 5, 6, 7, 8, 9))
+    group_send(2)
+    group_send(0)
 
     got = stat_wait(0)
     peak0 = jnp.max(jnp.max(got[:, 1:2, :], axis=0), axis=1, keepdims=True)
@@ -415,33 +421,34 @@
         for y in range(8):
             x2[z + 1, y + 1] = settle(r1[z, y], aff, b1)
 
-    def settle_halo(ph, raw, buf, zl, yl, which, aff, b):
+    def settle_halo(ph, raw, buf, which, aff, b):
         for i in which:
-            dz, dy = DIRS[i]
+            dz, dy = PIECES[ph][i][:2]
             there = exists(-dz, -dy)
+            zs, ys = halo_slots(ph, i)
 
             @pl.when(there)
             def _():
-                halo(ph, raw, zl, yl, i).wait_recv()
-                for z in slots(dz, zl):
-                    for y in slots(dy, yl):
+                halo(ph, raw, i).wait_recv()
+                for z in zs:
+                    for y in ys:
                         buf[z, y] = settle(raw[z, y].astype(F32), aff, b)
 
             @pl.when(jnp.logical_not(there))
             def _():
-                for z in slots(dz, zl):
-                    for y in slots(dy, yl):
+                for z in zs:
+                    for y in ys:
                         buf[z, y] = jnp.zeros(buf.shape[2:], buf.dtype)
 
     wb = wf2[...]
     acc = (zero, zero, None, None)
-    settle_halo(1, x2r, x2, 4, 8, (6, 7), aff, b1)
+    settle_halo(1, x2r, x2, (8, 9), aff, b1)
     for z in (1, 2):
         outs = fine_conv(x2, wb, z)
         acc = gather_stats(acc, outs, False)
         for y in range(8):
             r2[z, y] = outs[y]
-    settle_halo(1, x2r, x2, 4, 8, range(6), aff, b1)
+    settle_halo(1, x2r, x2, (0, 1, 4, 5, 6, 7, 2, 3, 10, 11), aff, b1)
 
     for z in (0, 3):
         outs = fine_conv(x2, wb, z)
@@ -477,7 +484,10 @@
         put_raw(blk, yp + 1, h3, z3s)
         hi = jnp.maximum(hi, blk)
         lo = jnp.minimum(lo, blk)
+    halo_done(0, x1)
     coarse_send(2, h3, z3s, z3r)
+    group_forward(2)
+    group_forward(0)
     group_send(1)
 
     got = stat_wait(1)
@@ -533,6 +543,7 @@
     for y in range(4):
         put_raw(outs[y], y + 1, h4, z4s)
         r4i[y] = outs[y]
+    halo_done(1, x2r)
     coarse_send(3, h4, z4s, z4r)
     group_forward(1)
 
@@ -566,12 +577,14 @@
 
     peaks = jnp.where(lane == 0, peak0, jnp.where(lane == 1, peak1, jnp.where(lane == 2, peak2, peak3)))
 
-    def cross(d, src):
+    def cross(src, dst, dev):
         return pltpu.make_async_remote_copy(
-            src_ref=am.at[smp], dst_ref=am.at[src],
-            send_sem=xs.at[d], recv_sem=xr.at[src],
-            device_id=other_sample(d)[1], device_id_type=MESH,
+            src_ref=am.at[src], dst_ref=am.at[dst], send_sem=xs.at[0], recv_sem=xs.at[1],
+            device_id=dev, device_id_type=MESH,
         )
+
+    def cross_all():
+        return cross(pl.ds(0, ns - 1), pl.ds(0, ns - 1), other_sample(1)[1])
 
     for y in range(4):
         c4[y + 1] = settle(r4i[y], aff3, b3)
@@ -579,17 +592,15 @@
     greeted(2)
     am[smp] = peaks
     for d in range(1, ns):
-        cross(d, smp).start()
+        cross(smp, smp, other_sample(d)[1]).start()
 
 
     group_wait(1)
     outs = coarse_conv(c4, c4z, wg4[...].reshape(192, 576))
     acc = gather_stats((zero64, zero64, None, None), outs, False)
-    def swap(d, src):
-        q = lax.rem(sy + d, ny)
+    def swap(src, dst, q):
         return pltpu.make_async_remote_copy(
-            src_ref=a2s.at[q], dst_ref=a2a.at[src],
-            send_sem=bs.at[d], recv_sem=br.at[src],
+            src_ref=a2s.at[src], dst_ref=a2a.at[dst], send_sem=bs.at[0], recv_sem=bs.at[1],
             device_id={"sy": q}, device_id_type=MESH,
         )
 
@@ -599,20 +610,18 @@
             a2s[g, y] = outs[y][16 * g : 16 * g + 16]
 
     for d in range(1, ny):
-        swap(d, sy).start()
+        q = lax.rem(sy + d, ny)
+        swap(q, sy, q).start()
+    swap_all = swap(pl.ds(0, ny - 1), pl.ds(0, ny - 1), mate)
     a2a[sy] = a2s[sy]
 
-    halo_done(0, x1, 4, 8)
-    halo_done(1, x2r, 4, 8)
     coarse_done(2, h3, z3s, z3r)
     coarse_done(3, h4, z4s, z4r)
     for ph in range(3):
-        for d in order:
-            stat_copy(ph, d, me).wait_send()
+        stat_all(ph).wait_send()
     for which in range(3):
         group_done(which)
-    for d in range(1, ny):
-        swap(d, lax.rem(sy + d, ny)).wait_recv()
+    swap_all.wait_recv()
     got = stat_wait(3)
     rows8b = to_cols(jnp.sum(got[:, 0:1, :], axis=0))
     gs[...] = rows8b
@@ -629,16 +638,14 @@
     both = [jnp.concatenate(planes[z], axis=1) for z in range(2)]
     coarse[...] = jnp.stack(both, axis=1).astype(BF16)
 
-    for d in range(1, ns):
-        cross(d, other_sample(d)[0]).wait_recv()
+    if ns > 1:
+        cross_all().wait_recv()
     amax[...] = jnp.max(am[...], axis=0)[:, 0:4]
 
-    for d in order:
-        stat_copy(3, d, me).wait_send()
-    for d in range(1, ny):
-        swap(d, sy).wait_send()
-    for d in range(1, ns):
-        cross(d, smp).wait_send()
+    stat_all(3).wait_send()
+    swap_all.wait_send()
+    if ns > 1:
+        cross_all().wait_send()
 
 
 def solution(mesh):
@@ -699,16 +706,14 @@
                 pltpu.VMEM((128, 128), F32),
                 pltpu.SemaphoreType.REGULAR((3,)),
                 dma((13,)),
-                dma((4, 8)),
-                dma((4, 8)),
-                dma((4, n)),
-                dma((4, n)),
+                dma((2, 12)),
+                dma((2, 12)),
+                dma((4,)),
+                dma((4,)),
                 dma((3, 3)),
                 dma((3, ny)),
-                dma((ny,)),
-                dma((ny,)),
-                dma((ns,)),
-                dma((ns,)),
+                dma((2,)),
+                dma((2,)),
             ],
             compiler_params=pltpu.CompilerParams(collective_id=0, has_side_effects=True),
             name="encoder",
@@ -748,7 +753,7 @@
         hist_v, gf_v, sf_v, gc_v, sc_v, vin, w1v, w2v, w3v, w4v, wf1, wf2, wg3, wg4,
         x1, r1, x2r, x2, r2, h3, z3s, z3r, p3, c3, c3z, h4, z4s, z4r, r4i, c4, c4z, a2a, a2s, grow,
         st, am, rows8, tcols,
-        rounds, lsem, hs, hr, ss, sr, ws, wr, bs, br, xs, xr,
+        rounds, lsem, hs, hr, ss, sr, ws, wr, bs, xs,
     ) = refs
     body(
         ny, nz, ns,
@@ -756,7 +761,7 @@
         hist_v, gf_v, sf_v, gc_v, sc_v, vin, w1v, w2v, w3v, w4v, wf1, wf2, wg3, wg4,
         x1, r1, x2r, x2, r2, h3, z3s, z3r, p3, c3, c3z, h4, z4s, z4r, r4i, c4, c4z, a2a, a2s, grow,
         st, am, rows8,
-        rounds, lsem, hs, hr, ss, sr, ws, wr, tcols, None, bs, br, xs, xr,
+        rounds, lsem, hs, hr, ss, sr, ws, wr, tcols, bs, xs,
     )
 
 

time: 42.8 us -> 40.4 us (0.944)
  Pallas kernels: 42 us -> 39.7 us
    pallas_call x1, Pallas kernels: 41.3 us -> 38.9 us  [step(): pl.pallas_call(functools.partial(body_entry, ny, nz, ns), out_shape=(pltp...]
where the time goes in v5:
time: 40.4 us; the launch traced here: 40.3 us
  Pallas kernels  39.7 us (98%)
  between operations  0.64 us (2%)
    pallas_call x1, Pallas kernels, step(): pl.pallas_call(functools.partial(body_entry, ny, nz, ns), out_shape=(pltp...  38.9 us

profile of v5, /device:TPU:1, one launch (start us, length us, event | category | flops | bytes accessed | tf_op | source)
XLA Modules:
  0.0 40.3 jit_solution(3575017496860371857)
XLA Ops:
  0.6 38.9 %encoder.1 = (bf16[4,32,8,128]{3,2,1,0:T(8,128)(2,1)S(1)}, bf16[16,2,1024]{2,1,0:T(2,128)(2,1)S(1)}, f32[1,4]{1,0:T(1,128)S(1)}) custom-call(bf16[32,4,8,128]{3,2,1,0:T(8,128)(2,1)} %bitcast.8, f32[4,16]{1,0:T(4,128)} %refs_1_.1, bf16[9,96,32]{2,1,0:T(8,128)(2,1)} %bitcast.9, bf16[9,96,32]{2,1,0:T(8,128)(2,1)} %bitcast.10, bf16[9,48,32]{2,1,0:T(8,128)(2,1)} %bitcast.11, ...), custom_call_target="tpu_custom_call" | custom-call | tf_op jit(solution)/shard_map/encoder/pallas_call | solution.py:659
  39.6 0.8 %emit.1 = (bf16[32,4,8,128]{3,2,1,0:T(8,128)(2,1)}, bf16[16,2,1024]{2,1,0:T(2,128)(2,1)}, f32[1,4]{1,0:T(1,128)}) custom-call(bf16[4,32,8,128]{3,2,1,0:T(8,128)(2,1)S(1)} %get-tuple-element.9.skip_v, bf16[16,2,1024]{2,1,0:T(2,128)(2,1)S(1)} %get-tuple-element.10.coarse_v, f32[1,4]{1,0:T(1,128)S(1)} %get-tuple-element.11.amax_v), custom_call_target="tpu_custom_call" | custom-call | tf_op jit(solution)/shard_map/emit/pallas_call | solution.py:724

commit v6 on v5

--- a/solution.py
+++ b/solution.py
@@ -26,7 +26,7 @@
     vol, hist_h, w1, w2, w3, w4, gf_h, sf_h, gc_h, sc_h,
     skip, coarse, amax,
     hist, gf, sf, gc, sc, vin, w1v, w2v, w3v, w4v, wf1, wf2, wg3, wg4,
-    x1, r1, x2r, x2, r2, h3, z3s, z3r, p3, c3, c3z, h4, z4s, z4r, r4i, c4, c4z, a2a, a2s, grow,
+    x1, r1, x2r, x2, r2, h3, z3s, z3r, p3, c3, c3z, h4, z4s, z4r, r4i, c4, c4z, a2a, a2s,
     st, am, rows8,
     rounds, lsem, hs, hr, ss, sr, ws, wr, gs, bs, xs,
 ):
@@ -53,10 +53,11 @@
     def greeted(r):
         pl.semaphore_wait(rounds.at[r], len(near))
 
-    loads = [pltpu.make_async_copy(vol.at[:, z], vin.at[z], lsem.at[z]) for z in range(4)]
+    place = {0: 0, 3: 1, 1: 2, 2: 3}
+    loads = [pltpu.make_async_copy(vol.at[:, z], vin.at[place[z]], lsem.at[place[z] // 2]) for z in range(4)]
     small = ((hist_h, hist), (w1, w1v), (w2, w2v), (w3, w3v), (w4, w4v), (gf_h, gf), (sf_h, sf), (gc_h, gc), (sc_h, sc))
     for i, (s, d) in enumerate(small):
-        loads.append(pltpu.make_async_copy(s, d, lsem.at[4 + i]))
+        loads.append(pltpu.make_async_copy(s, d, lsem.at[2 + i]))
     for i in (4, 0, 3, 1, 2, 5, 6, 7, 8, 9, 10, 11, 12):
         loads[i].start()
 
@@ -96,7 +97,7 @@
         return pltpu.make_async_remote_copy(
             src_ref=buf.at[src_z(dz, 4), pl.ds(row, count)],
             dst_ref=buf.at[dst_z(dz, 4), pl.ds(row - 8 * dy, count)],
-            send_sem=hs.at[ph % 2, i],
+            send_sem=hs.at[i],
             recv_sem=hr.at[ph % 2, i],
             device_id={"sy": sy + dy, "sz": sz + dz},
             device_id_type=MESH,
@@ -114,8 +115,8 @@
             def _():
                 halo(ph, buf, i).wait_recv()
 
-    def halo_done(ph, buf):
-        for i in range(len(PIECES[ph])):
+    def halo_done(ph, buf, which):
+        for i in which:
             @pl.when(exists(*PIECES[ph][i][:2]))
             def _():
                 halo(ph, buf, i).wait_send()
@@ -132,7 +133,7 @@
             up = 1 if dz > 0 else 0
             src, dst = zs.at[up, src_z(dy, 4)], zr.at[1 - up, dst_z(dy, 4)]
         return pltpu.make_async_remote_copy(
-            src_ref=src, dst_ref=dst, send_sem=hs.at[ph % 2, i], recv_sem=hr.at[ph % 2, i],
+            src_ref=src, dst_ref=dst, send_sem=hs.at[i], recv_sem=hr.at[ph % 2, i],
             device_id={"sy": sy + dy, "sz": sz + dz}, device_id_type=MESH,
         )
 
@@ -188,7 +189,7 @@
     def stat_copy(ph, src, dst, dev):
         return pltpu.make_async_remote_copy(
             src_ref=st.at[ph, src], dst_ref=st.at[ph, dst],
-            send_sem=ss.at[ph], recv_sem=sr.at[ph],
+            send_sem=ss.at[0], recv_sem=sr.at[ph % 2],
             device_id=dev, device_id_type=MESH,
         )
 
@@ -197,6 +198,8 @@
         return stat_copy(ph, rest, rest, partner(1)[1])
 
     def stat_send(ph, rows):
+        if ph > 0:
+            stat_all(ph - 1).wait_send()
         st[ph, me] = jnp.concatenate(rows + [rows[0]] * (4 - len(rows)), axis=0)
         for d in order:
             stat_copy(ph, me, me, partner(d)[1]).start()
@@ -236,9 +239,10 @@
 
     def take(zp):
         parts = []
+        pair = pl.ds(place[zp[0]], 2)
+        pltpu.make_async_copy(vin.at[pair], vin.at[pair], lsem.at[place[zp[0]] // 2]).wait()
         for z in zp:
-            loads[z].wait()
-            v = vin[z].astype(F32).reshape(256, 128)
+            v = vin[place[z]].astype(F32).reshape(256, 128)
             peaks0.append(jnp.abs(v))
             parts.append(v.astype(BF16))
         moved = jnp.dot(into, jnp.concatenate(parts, axis=1), preferred_element_type=F32)
@@ -276,8 +280,6 @@
     wf2[...] = lanes_of(w2v)
     wg3[sy] = lanes_of(w3v)
     wg4[sy] = lanes_of(w4v)
-    grow[sy, 0] = rows8[4]
-    grow[sy, 1] = rows8[6]
 
     for i in range(len(PIECES[0])):
         @pl.when(jnp.logical_not(exists(-PIECES[0][i][0], -PIECES[0][i][1])))
@@ -291,10 +293,10 @@
     cross_mate = lax.rem(mate + 2, 4)
 
     def group(which, kind, src):
-        buf = (wg3, wg4, grow)[which]
+        buf = (wg3, wg4)[which]
         return pltpu.make_async_remote_copy(
             src_ref=buf.at[src], dst_ref=buf.at[src],
-            send_sem=ws.at[which, kind], recv_sem=wr.at[which, src],
+            send_sem=ws.at[which, kind], recv_sem=wr.at[which, kind],
             device_id={"sy": cross_sy if kind == 1 else mate}, device_id_type=MESH,
         )
 
@@ -392,6 +394,7 @@
     halo_wait(0, x1, (0, 1))
     for z in (0, 3):
         acc = first_rows(z, (1, 2, 3, 4), acc)
+    halo_done(0, x1, (0, 1))
     halo_send(1, x2r, (0, 1))
     halo_wait(0, x1, (8, 9))
     for z in (1, 2):
@@ -402,12 +405,13 @@
     row = mixed_row(jnp.concatenate(acc, axis=0))
     greeted(1)
     greet(2)
-    stat_send(0, [row, jnp.broadcast_to(peak0, (1, 128))])
+    stat_send(0, [row, jnp.broadcast_to(peak0, (1, 128)), rows8[4:5], rows8[6:7]])
+    halo_done(0, x1, range(2, 10))
     halo_send(1, x2r, (2, 3, 10, 11, 4, 5, 6, 7, 8, 9))
-    group_send(2)
     group_send(0)
 
     got = stat_wait(0)
+    group_send(1)
     peak0 = jnp.max(jnp.max(got[:, 1:2, :], axis=0), axis=1, keepdims=True)
     cols = mixed_total(got)
     aff = fine_affine(cols, 0)
@@ -417,9 +421,6 @@
     def settle(v, aff, b):
         return jnp.clip(act(v, aff), -b, b).astype(BF16)
 
-    for z in range(4):
-        for y in range(8):
-            x2[z + 1, y + 1] = settle(r1[z, y], aff, b1)
 
     def settle_halo(ph, raw, buf, which, aff, b):
         for i in which:
@@ -443,6 +444,9 @@
     wb = wf2[...]
     acc = (zero, zero, None, None)
     settle_halo(1, x2r, x2, (8, 9), aff, b1)
+    for z in range(4):
+        for y in range(8):
+            x2[z + 1, y + 1] = settle(r1[z, y], aff, b1)
     for z in (1, 2):
         outs = fine_conv(x2, wb, z)
         acc = gather_stats(acc, outs, False)
@@ -484,18 +488,15 @@
         put_raw(blk, yp + 1, h3, z3s)
         hi = jnp.maximum(hi, blk)
         lo = jnp.minimum(lo, blk)
-    halo_done(0, x1)
+    halo_done(1, x2r, range(12))
     coarse_send(2, h3, z3s, z3r)
-    group_forward(2)
     group_forward(0)
-    group_send(1)
+    group_forward(1)
 
     got = stat_wait(1)
     cols = to_cols(jnp.sum(got[:, 0:1, :], axis=0))
     aff2 = fine_affine(cols, 1)
     b2 = bound_of(2)
-    for yp in range(4):
-        c3[yp + 1] = settle(p3[yp], aff2, b2)
     coarse_settle(2, h3, z3s, z3r, c3, c3z, aff2, b2)
 
     cfirst, clast = (lane & 63) == 0, (lane & 63) == 63
@@ -530,6 +531,8 @@
         return outs
 
     group_wait(0)
+    for yp in range(4):
+        c3[yp + 1] = settle(p3[yp], aff2, b2)
     outs = coarse_conv(c3, c3z, wg3[...].reshape(192, 288))
     zero64 = jnp.zeros((64, 128), F32)
     acc = (zero64, zero64, jnp.full((64, 128), -jnp.inf, F32), jnp.full((64, 128), jnp.inf, F32))
@@ -543,9 +546,8 @@
     for y in range(4):
         put_raw(outs[y], y + 1, h4, z4s)
         r4i[y] = outs[y]
-    halo_done(1, x2r)
+    coarse_done(2, h3, z3s, z3r)
     coarse_send(3, h4, z4s, z4r)
-    group_forward(1)
 
     outof = onehot(jnp.logical_and((ci & 31) == (ri >> 3), (ci >> 5) == (ri & 7)))
     for zp in range(2):
@@ -557,8 +559,7 @@
             z = 2 * zp + k
             skip[z] = moved[:, 128 * k : 128 * k + 128].reshape(32, 8, 128).astype(BF16)
 
-    group_wait(2)
-    gall = jnp.transpose(grow[...].reshape(2 * ny, 128))
+    gall = jnp.transpose(jnp.concatenate([st[0, sz * ny + g, 2:4] for g in range(ny)], axis=0))
 
     def gathered(k):
         parts = [gall[0:16, 2 * g + k : 2 * g + k + 1] for g in range(ny)]
@@ -566,36 +567,37 @@
 
     got = stat_wait(2)
     cols = to_cols(jnp.sum(got[:, 0:1, :], axis=0))
+    aff3 = affine(cols[0:64], cols[64:128], coarse_cells, gathered(0), gathered(1))
+    b3 = bound_of(3)
+
+    def cross(src, dst, dev):
+        return pltpu.make_async_remote_copy(
+            src_ref=am.at[src], dst_ref=am.at[dst], send_sem=xs.at[0], recv_sem=xs.at[1],
+            device_id=dev, device_id_type=MESH,
+        )
+
+    def cross_all():
+        return cross(pl.ds(0, ns - 1), pl.ds(0, ns - 1), other_sample(1)[1])
+
+    coarse_settle(3, h4, z4s, z4r, c4, c4z, aff3, b3)
+    group_wait(1)
+    for y in range(4):
+        c4[y + 1] = settle(r4i[y], aff3, b3)
+
     high = jnp.max(got[:, 1:3, :], axis=0)
     low = jnp.min(got[:, 1:3, :], axis=0)
     ext = jnp.where(lower, high, low)
     pext, ext = to_cols(ext[1:2]), to_cols(ext[0:1])
     peak2 = peak_of(pext[0:32], pext[64:96], aff2)
-    aff3 = affine(cols[0:64], cols[64:128], coarse_cells, gathered(0), gathered(1))
     peak3 = peak_of(ext[0:64], ext[64:128], aff3)
-    b3 = bound_of(3)
-
     peaks = jnp.where(lane == 0, peak0, jnp.where(lane == 1, peak1, jnp.where(lane == 2, peak2, peak3)))
 
-    def cross(src, dst, dev):
-        return pltpu.make_async_remote_copy(
-            src_ref=am.at[src], dst_ref=am.at[dst], send_sem=xs.at[0], recv_sem=xs.at[1],
-            device_id=dev, device_id_type=MESH,
-        )
-
-    def cross_all():
-        return cross(pl.ds(0, ns - 1), pl.ds(0, ns - 1), other_sample(1)[1])
-
-    for y in range(4):
-        c4[y + 1] = settle(r4i[y], aff3, b3)
-    coarse_settle(3, h4, z4s, z4r, c4, c4z, aff3, b3)
     greeted(2)
     am[smp] = peaks
     for d in range(1, ns):
         cross(smp, smp, other_sample(d)[1]).start()
 
 
-    group_wait(1)
     outs = coarse_conv(c4, c4z, wg4[...].reshape(192, 576))
     acc = gather_stats((zero64, zero64, None, None), outs, False)
     def swap(src, dst, q):
@@ -607,7 +609,7 @@
     stat_send(3, [sum_row(acc[0:2])])
     for g in range(4):
         for y in range(4):
-            a2s[g, y] = outs[y][16 * g : 16 * g + 16]
+            a2s[g, y] = outs[y][16 * g : 16 * g + 16].astype(BF16)
 
     for d in range(1, ny):
         q = lax.rem(sy + d, ny)
@@ -615,11 +617,8 @@
     swap_all = swap(pl.ds(0, ny - 1), pl.ds(0, ny - 1), mate)
     a2a[sy] = a2s[sy]
 
-    coarse_done(2, h3, z3s, z3r)
     coarse_done(3, h4, z4s, z4r)
-    for ph in range(3):
-        stat_all(ph).wait_send()
-    for which in range(3):
+    for which in range(2):
         group_done(which)
     swap_all.wait_recv()
     got = stat_wait(3)
@@ -631,8 +630,8 @@
     planes = [[], []]
     for g in range(4):
         for yp in range(2):
-            u = act(a2a[g, 2 * yp], aff4)
-            v = act(a2a[g, 2 * yp + 1], aff4)
+            u = act(a2a[g, 2 * yp].astype(F32), aff4)
+            v = act(a2a[g, 2 * yp + 1].astype(F32), aff4)
             planes[0].append(jnp.where(lower, u, pltpu.roll(v, 64, 1)))
             planes[1].append(jnp.where(lower, pltpu.roll(u, 64, 1), v))
     both = [jnp.concatenate(planes[z], axis=1) for z in range(2)]
@@ -697,21 +696,20 @@
                 pltpu.VMEM((4, 64, 128), F32),
                 pltpu.VMEM((6, 64, 128), BF16),
                 pltpu.VMEM((2, 6, 32, 128), BF16),
-                pltpu.VMEM((ny, 4, 16, 128), F32),
-                pltpu.VMEM((ny, 4, 16, 128), F32),
-                pltpu.VMEM((ny, 2, 128), F32),
+                pltpu.VMEM((ny, 4, 16, 128), BF16),
+                pltpu.VMEM((ny, 4, 16, 128), BF16),
                 pltpu.VMEM((4, n, 4, 128), F32),
                 pltpu.VMEM((ns, 1, 128), F32),
                 pltpu.VMEM((8, 128), F32),
                 pltpu.VMEM((128, 128), F32),
                 pltpu.SemaphoreType.REGULAR((3,)),
-                dma((13,)),
+                dma((11,)),
+                dma((12,)),
                 dma((2, 12)),
-                dma((2, 12)),
-                dma((4,)),
-                dma((4,)),
-                dma((3, 3)),
-                dma((3, ny)),
+                dma((1,)),
+                dma((2,)),
+                dma((2, 3)),
+                dma((2, 3)),
                 dma((2,)),
                 dma((2,)),
             ],
@@ -751,7 +749,7 @@
     (
         vol, hist, w1, w2, w3, w4, gf, sf, gc, sc, skip, coarse, amax,
         hist_v, gf_v, sf_v, gc_v, sc_v, vin, w1v, w2v, w3v, w4v, wf1, wf2, wg3, wg4,
-        x1, r1, x2r, x2, r2, h3, z3s, z3r, p3, c3, c3z, h4, z4s, z4r, r4i, c4, c4z, a2a, a2s, grow,
+        x1, r1, x2r, x2, r2, h3, z3s, z3r, p3, c3, c3z, h4, z4s, z4r, r4i, c4, c4z, a2a, a2s,
         st, am, rows8, tcols,
         rounds, lsem, hs, hr, ss, sr, ws, wr, bs, xs,
     ) = refs
@@ -759,7 +757,7 @@
         ny, nz, ns,
         vol, hist, w1, w2, w3, w4, gf, sf, gc, sc, skip, coarse, amax,
         hist_v, gf_v, sf_v, gc_v, sc_v, vin, w1v, w2v, w3v, w4v, wf1, wf2, wg3, wg4,
-        x1, r1, x2r, x2, r2, h3, z3s, z3r, p3, c3, c3z, h4, z4s, z4r, r4i, c4, c4z, a2a, a2s, grow,
+        x1, r1, x2r, x2, r2, h3, z3s, z3r, p3, c3, c3z, h4, z4s, z4r, r4i, c4, c4z, a2a, a2s,
         st, am, rows8,
         rounds, lsem, hs, hr, ss, sr, ws, wr, tcols, bs, xs,
     )

time: 40.4 us -> 40.4 us (level)
  no operation moved by 1% of the time
where the time goes in v6:
time: 40.4 us; the launch traced here: 40.3 us
  Pallas kernels  39.7 us (98%)
  between operations  0.64 us (2%)
    pallas_call x1, Pallas kernels, step(): pl.pallas_call(functools.partial(body_entry, ny, nz, ns), out_shape=(pltp...  38.9 us

profile of v6, /device:TPU:1, one launch (start us, length us, event | category | flops | bytes accessed | tf_op | source)
XLA Modules:
  0.0 40.3 jit_solution(6449815229552782658)
XLA Ops:
  0.6 38.9 %encoder.1 = (bf16[4,32,8,128]{3,2,1,0:T(8,128)(2,1)S(1)}, bf16[16,2,1024]{2,1,0:T(2,128)(2,1)S(1)}, f32[1,4]{1,0:T(1,128)S(1)}) custom-call(bf16[32,4,8,128]{3,2,1,0:T(8,128)(2,1)} %bitcast.8, f32[4,16]{1,0:T(4,128)} %refs_1_.1, bf16[9,96,32]{2,1,0:T(8,128)(2,1)} %bitcast.9, bf16[9,96,32]{2,1,0:T(8,128)(2,1)} %bitcast.10, bf16[9,48,32]{2,1,0:T(8,128)(2,1)} %bitcast.11, ...), custom_call_target="tpu_custom_call" | custom-call | tf_op jit(solution)/shard_map/encoder/pallas_call | solution.py:658
  39.5 0.8 %emit.1 = (bf16[32,4,8,128]{3,2,1,0:T(8,128)(2,1)}, bf16[16,2,1024]{2,1,0:T(2,128)(2,1)}, f32[1,4]{1,0:T(1,128)}) custom-call(bf16[4,32,8,128]{3,2,1,0:T(8,128)(2,1)S(1)} %get-tuple-element.9.skip_v, bf16[16,2,1024]{2,1,0:T(2,128)(2,1)S(1)} %get-tuple-element.10.coarse_v, f32[1,4]{1,0:T(1,128)S(1)} %get-tuple-element.11.amax_v), custom_call_target="tpu_custom_call" | custom-call | tf_op jit(solution)/shard_map/emit/pallas_call | solution.py:722

commit v7 on v6

--- a/solution.py
+++ b/solution.py
@@ -400,15 +400,15 @@
     for z in (1, 2):
         acc = first_rows(z, range(8), acc)
     halo_wait(0, x1, range(2, 8))
+    greeted(1)
     for z in (0, 3):
         acc = first_rows(z, (0, 5, 6, 7), acc)
     row = mixed_row(jnp.concatenate(acc, axis=0))
-    greeted(1)
-    greet(2)
     stat_send(0, [row, jnp.broadcast_to(peak0, (1, 128)), rows8[4:5], rows8[6:7]])
     halo_done(0, x1, range(2, 10))
     halo_send(1, x2r, (2, 3, 10, 11, 4, 5, 6, 7, 8, 9))
     group_send(0)
+    greet(2)
 
     got = stat_wait(0)
     group_send(1)

time: 40.4 us -> 40.4 us (level)
  no operation moved by 1% of the time
where the time goes in v7:
time: 40.4 us; the launch traced here: 40.3 us
  Pallas kernels  39.7 us (98%)
  between operations  0.64 us (2%)
    pallas_call x1, Pallas kernels, step(): pl.pallas_call(functools.partial(body_entry, ny, nz, ns), out_shape=(pltp...  38.9 us

profile of v7, /device:TPU:1, one launch (start us, length us, event | category | flops | bytes accessed | tf_op | source)
XLA Modules:
  0.0 40.3 jit_solution(14480606680013949159)
XLA Ops:
  0.6 38.9 %encoder.1 = (bf16[4,32,8,128]{3,2,1,0:T(8,128)(2,1)S(1)}, bf16[16,2,1024]{2,1,0:T(2,128)(2,1)S(1)}, f32[1,4]{1,0:T(1,128)S(1)}) custom-call(bf16[32,4,8,128]{3,2,1,0:T(8,128)(2,1)} %bitcast.8, f32[4,16]{1,0:T(4,128)} %refs_1_.1, bf16[9,96,32]{2,1,0:T(8,128)(2,1)} %bitcast.9, bf16[9,96,32]{2,1,0:T(8,128)(2,1)} %bitcast.10, bf16[9,48,32]{2,1,0:T(8,128)(2,1)} %bitcast.11, ...), custom_call_target="tpu_custom_call" | custom-call | tf_op jit(solution)/shard_map/encoder/pallas_call | solution.py:658
  39.6 0.8 %emit.1 = (bf16[32,4,8,128]{3,2,1,0:T(8,128)(2,1)}, bf16[16,2,1024]{2,1,0:T(2,128)(2,1)}, f32[1,4]{1,0:T(1,128)}) custom-call(bf16[4,32,8,128]{3,2,1,0:T(8,128)(2,1)S(1)} %get-tuple-element.9.skip_v, bf16[16,2,1024]{2,1,0:T(2,128)(2,1)S(1)} %get-tuple-element.10.coarse_v, f32[1,4]{1,0:T(1,128)S(1)} %get-tuple-element.11.amax_v), custom_call_target="tpu_custom_call" | custom-call | tf_op jit(solution)/shard_map/emit/pallas_call | solution.py:722
